TPU v7x, 128 devices: a whole 4x4x4 slice. The times are simulated.
128 devices in a mesh: gx: 16 (over z, x), gy: 8 (over y, core).
Axes of the slice: x: 4, y: 4, z: 4, core: 2. Of those that a mesh axis runs over, the one named last changes fastest.
Arguments:
- density: float32 [1024, 256, 128], P('gx', 'gy'), may hold values from -6 to 6
- slowness: float32 [1024, 256, 128], P('gx', 'gy'), may hold values from -6 to 6
- pressure_obs: float32 [1024, 256, 128], P('gx', 'gy'), may hold values from -6 to 6
- time_obs: float32 [1024, 256, 128], P('gx', 'gy'), may hold values from -6 to 6
- zone_map: int32 [1024, 256, 128], P('gx', 'gy'), may hold values from 0 to 7
- zone_low: float32 [8], replicated, may hold values from -2.5 to -0.5
- zone_high: float32 [8], replicated, may hold values from 0.5 to 2.5
Outputs:
- density_out: float32 [1024, 256, 128], P('gx', 'gy')
- slowness_out: float32 [1024, 256, 128], P('gx', 'gy')
- objective: float32 [3], replicated
All inputs are finite; a program needn't handle non-finite values.
Results may differ from a plain program's by a relative error of at most 0.00013.
Values sent between devices are 32-bit elements; how exact they have to be, the bound alone decides.
A program may use at most 128 MiB of HBM per device.

v0:
```python
import math

import jax
import jax.numpy as jnp
from jax import lax
from jax.sharding import Mesh
from jax.sharding import PartitionSpec as P

ITERS = 3
GX_GY = ("gx_0", "gx_1", "gy_0", "gy_1")
GX = ("gx_0", "gx_1")
GY = ("gy_0", "gy_1")


BETA = 1.0
ETA = 0.5
EPSILON = 1e-06


def over_axes(value, axes):
    for axis in axes:
        value = lax.psum(value, axis)
    return value


def laid_out(tiles, dim):
    tiles = jnp.moveaxis(tiles, 0, dim)
    dims = tiles.shape
    return tiles.reshape(*dims[:dim], dims[dim] * dims[dim + 1], *dims[dim + 2 :])


def copy_for_each(value, axis):
    copies = jnp.broadcast_to(value, (lax.axis_size(axis), *value.shape))
    return lax.all_to_all(copies, axis, split_axis=0, concat_axis=0, tiled=True)


def collect(value, axis, dim):
    return laid_out(copy_for_each(value, axis), dim)


def with_halo(value, sides, width):
    for axis, dim in sides:
        size, length = (lax.axis_size(axis), value.shape[dim])
        up = [(i, (i + 1) % size) for i in range(size - 1)]
        down = [(j, i) for i, j in up]
        last = lax.slice_in_dim(value, length - width, length, axis=dim)
        initial = lax.slice_in_dim(value, 0, width, axis=dim)
        before = lax.ppermute(last, axis, up)
        after = lax.ppermute(initial, axis, down)
        value = jnp.concatenate([before, value, after], axis=dim)
    return value


def cross_product(first_vec, second_vec):
    return (
        first_vec[1] * second_vec[2] - first_vec[2] * second_vec[1],
        first_vec[2] * second_vec[0] - first_vec[0] * second_vec[2],
        first_vec[0] * second_vec[1] - first_vec[1] * second_vec[0],
    )


def depth_slope(inner):
    padded = jnp.pad(inner, [(0, 0)] * (inner.ndim - 1) + [(1, 1)])
    return (padded[..., 2:] - padded[..., :-2]) * 0.5


def depth_adjoint(values):
    padded = jnp.pad(values, [(0, 0)] * (values.ndim - 1) + [(1, 1)])
    return (padded[..., :-2] - padded[..., 2:]) * 0.5


def block_slopes(padded):
    along_x = (padded[:, 2:, 1:-1] - padded[:, :-2, 1:-1]) * 0.5
    along_y = (padded[:, 1:-1, 2:] - padded[:, 1:-1, :-2]) * 0.5
    along_z = depth_slope(padded[:, 1:-1, 1:-1])
    return (along_x, along_y, along_z)


def triangle(length, upward):
    first = jnp.arange(length)[:, None]
    second = jnp.arange(length)[None, :]
    if upward:
        return (first <= second).astype(jnp.float32)
    return (first >= second).astype(jnp.float32)


def depth_prefix(values, upward):
    table = triangle(values.shape[-1], upward)
    return jnp.einsum("xyj,jk->xyk", values, table, precision=lax.Precision.HIGHEST)


def rows_prefix(values, upward):
    table = triangle(values.shape[0], not upward)
    return jnp.einsum("ij,jyz->iyz", table, values, precision=lax.Precision.HIGHEST)


def global_sums(values):
    return (over_axes(values[0], GX_GY), over_axes(values[1], GX_GY), over_axes(values[2], GX_GY))


def local(density, slowness, pressure_obs, time_obs, zone_map, zone_low, zone_high):
    size_x, size_y, depth = density.shape
    parts_x = lax.axis_size(GX)
    parts_y = lax.axis_size(GY)
    total_x = size_x * parts_x
    total_y = size_y * parts_y
    cells = float(total_x * total_y * depth)
    zscale = 1.0 / math.sqrt(depth)
    xscale = 1.0 / math.sqrt(total_x)
    lower_bound = jnp.zeros(density.shape, jnp.float32)
    upper_bound = jnp.zeros(density.shape, jnp.float32)
    for zone_index in range(zone_low.shape[0]):
        hit = zone_map == zone_index
        lower_bound = jnp.where(hit, zone_low[zone_index], lower_bound)
        upper_bound = jnp.where(hit, zone_high[zone_index], upper_bound)
    my_x = lax.axis_index(GX)
    my_y = lax.axis_index(GY)
    anchor_x = my_x * size_x
    anchor_y = my_y * size_y
    shard_ids = jnp.arange(parts_x)
    own_weight = (shard_ids == my_x).astype(jnp.float32)
    later_weight = (shard_ids > my_x).astype(jnp.float32)
    earlier_table = (shard_ids[:, None] > shard_ids[None, :]).astype(jnp.float32)
    observed_totals = collect(jnp.sum(time_obs, 0)[None], GX, 0)
    observed_later = jnp.einsum(
        "k,kyz->yz", later_weight, observed_totals, precision=lax.Precision.HIGHEST
    )
    density_now = density
    slowness_now = slowness
    history = []
    for iteration in range(ITERS):
        fields = jnp.stack((density_now, slowness_now))
        padded = with_halo(fields, ((GX, 1), (GY, 2)), 2)
        along_x, along_y, along_z = block_slopes(padded)
        first_vec = (along_x[0], along_y[0], along_z[0])
        second_vec = (along_x[1], along_y[1], along_z[1])
        crossed_wide = cross_product(first_vec, second_vec)
        toward_density = cross_product(second_vec, crossed_wide)
        toward_slowness = cross_product(crossed_wide, first_vec)
        rows_x = anchor_x - 1 + jnp.arange(size_x + 2)
        rows_y = anchor_y - 1 + jnp.arange(size_y + 2)
        inside_x = (rows_x >= 0) & (rows_x < total_x)
        inside_y = (rows_y >= 0) & (rows_y < total_y)
        inside = (inside_x[:, None] & inside_y[None, :]).astype(jnp.float32)[:, :, None]
        side_x = jnp.stack((toward_density[0], toward_slowness[0])) * inside
        side_y = jnp.stack((toward_density[1], toward_slowness[1])) * inside
        back_x = (side_x[:, :-2, 1:-1] - side_x[:, 2:, 1:-1]) * 0.5
        back_y = (side_y[:, 1:-1, :-2] - side_y[:, 1:-1, 2:]) * 0.5
        depth_parts = jnp.stack((toward_density[2], toward_slowness[2]))[:, 1:-1, 1:-1]
        back_z = depth_adjoint(depth_parts)
        crossed = tuple((member[1:-1, 1:-1] for member in crossed_wide))
        cross_term = back_x + back_y + back_z
        pressure_miss = depth_prefix(density_now, True) * zscale - pressure_obs
        running = rows_prefix(slowness_now, True)
        stacked = jnp.stack((running[-1], jnp.sum(running, 0)))[None]
        gathered = collect(stacked, GX, 0)
        befores = jnp.einsum(
            "kj,jyz->kyz", earlier_table, gathered[:, 0], precision=lax.Precision.HIGHEST
        )
        before = jnp.einsum("k,kyz->yz", own_weight, befores, precision=lax.Precision.HIGHEST)
        shard_sums = gathered[:, 1] + float(size_x) * befores
        after_early = (
            jnp.einsum("k,kyz->yz", later_weight, shard_sums, precision=lax.Precision.HIGHEST)
            * xscale
            - observed_later
        )
        time_miss = (running + before[None]) * xscale - time_obs
        backward = rows_prefix(time_miss, False)
        column_back = depth_prefix(pressure_miss, False)
        grad_density = column_back * zscale + BETA * cross_term[0]
        grad_slowness = (backward + after_early[None]) * xscale + BETA * cross_term[1]
        crossed_sq = (
            jnp.sum(crossed[0] * crossed[0])
            + jnp.sum(crossed[1] * crossed[1])
            + jnp.sum(crossed[2] * crossed[2])
        )
        local_objective = (
            0.5
            * (
                jnp.sum(pressure_miss * pressure_miss)
                + jnp.sum(time_miss * time_miss)
                + BETA * crossed_sq
            )
            / cells
        )
        local_density = jnp.sum(grad_density * grad_density)
        local_slowness = jnp.sum(grad_slowness * grad_slowness)
        objective_now, norm_density, norm_slowness = global_sums(
            (local_objective, local_density, local_slowness)
        )
        history.append(objective_now)
        moved = density_now - ETA * grad_density * lax.rsqrt(norm_density / cells + EPSILON)
        density_now = jnp.minimum(jnp.maximum(moved, lower_bound), upper_bound)
        slowness_now = slowness_now - ETA * grad_slowness * lax.rsqrt(
            norm_slowness / cells + EPSILON
        )
    objective = jnp.stack(history)
    return (density_now, slowness_now, objective)


def solution(mesh):
    torus = Mesh(mesh.devices.reshape(4, 4, 4, 2), ("gx_0", "gx_1", "gy_0", "gy_1"))
    in_specs = (
        P(GX, GY, None),
        P(GX, GY, None),
        P(GX, GY, None),
        P(GX, GY, None),
        P(GX, GY, None),
        P(),
        P(),
    )
    out_specs = (P(GX, GY, None), P(GX, GY, None), P())
    return jax.shard_map(local, mesh=torus, in_specs=in_specs, out_specs=out_specs, check_vma=False)
```

profile of v0, /device:TPU:1, one launch (start us, length us, event | category | flops | bytes accessed | tf_op | source)
XLA Modules:
  0.0 323.9 jit_solution(1561969263531289439)
XLA Ops:
  1.6 3.9 %collective-permute-start = (f32[2,2,32,128]{3,2,1,0:T(8,128)S(1)}, f32[2,2,32,128]{3,2,1,0:T(8,128)S(1)}, u32[]{:S(2)}, u32[]{:S(2)}) collective-permute-start(f32[2,2,32,128]{3,2,1,0:T(8,128)S(1)} %get-tuple-element.91), channel_id=1, source_target_pairs={{0,8},{8,16},{16,24},{24,32},{32,40},{40,48},{48,56},{56,64},{64,7... | collective-permute-start | bytes 196616 | tf_op jit(solution)/shard_map/ppermute | solution.py:48
  10.1 8.5 %all-to-all-start = ((f32[16,1,2,32,128]{4,3,2,1,0:T(8,128)}), f32[16,1,2,32,128]{4,3,2,1,0:T(8,128)}, u32[]{:S(2)}, u32[]{:S(2)}) async-start(f32[16,1,2,32,128]{4,3,2,1,0:T(8,128)} %broadcast_in_dim.119), calls=%async_computation | async-start | bytes 1048576 | tf_op jit(solution)/shard_map/all_to_all | solution.py:34
  18.7 3.4 %multiply_reduce_fusion.5 = (f32[]{:T(128)}, f32[64,32,128]{2,0,1:T(8,128)}) fusion(f32[64,32,128]{2,1,0:T(8,128)S(1)} %copy-done.6, f32[64,32,128]{2,1,0:T(8,128)S(1)} %copy-done.1), kind=kOutput, calls=%fused_computation.182 | convolution fusion | flops 403718144 | bytes 3145732 | tf_op jit(solution)/shard_map/xyj,jk->xyk/dot_general | solution.py:89
  22.1 2.2 broadcast_compare_fusion
  24.5 4.6 %collective-permute-start.3 = (f32[2,68,2,128]{3,2,1,0:T(2,128)S(1)}, f32[2,68,2,128]{3,2,1,0:T(2,128)S(1)}, u32[]{:S(2)}, u32[]{:S(2)}) collective-permute-start(f32[2,68,2,128]{3,2,1,0:T(2,128)S(1)} %get-tuple-element.85), channel_id=1, source_target_pairs={{0,1},{1,2},{2,3},{3,4},{4,5},{5,6},{6,7},{8,9},{9,10},{10,11},{11... | collective-permute-start | bytes 417800 | tf_op jit(solution)/shard_map/ppermute | solution.py:48
  29.1 2.4 collective-permute-start.2
  32.8 2.6 collective-permute-done.2
  41.4 1.8 multiply_subtract_fusion.19
  45.6 2.2 fusion.23
  51.5 4.1 %multiply_reduce_fusion.11 = (f32[]{:T(128)}, f32[64,32,128]{2,1,0:T(8,128)}) fusion(f32[2,64,32,128]{3,2,1,0:T(8,128)} %fusion.23, f32[64,32,128]{2,0,1:T(8,128)S(1)} %copy-done.24), kind=kOutput, calls=%fused_computation.196 | convolution fusion | flops 403718144 | bytes 3145732 | tf_op jit(solution)/shard_map/xyj,jk->xyk/dot_general | solution.py:89
  57.8 3.9 %multiply_reduce_fusion.4 = (f32[]{:T(128)}, f32[64,32,128]{2,1,0:T(8,128)}, f32[32,128]{1,0:T(8,128)S(1)}) fusion(f32[64,32,128]{2,1,0:T(8,128)} %param.10, f32[32,128]{1,0:T(8,128)S(1)} %bitcast.239, f32[64,32,128]{2,0,1:T(8,128)} %copy-done.19), kind=kLoop, calls=%fused_computation.181 | loop fusion | flops 1568767 | bytes 3178500 | tf_op jit(solution)/shard_map/reduce_sum | solution.py:181
  62.5 7.1 %all-to-all-start.1 = ((f32[16,1,32,128]{3,2,1,0:T(8,128)}), f32[16,1,32,128]{3,2,1,0:T(8,128)}, u32[]{:S(2)}, u32[]{:S(2)}) async-start(f32[16,1,32,128]{3,2,1,0:T(8,128)} %broadcast_in_dim.120), calls=%async_computation.1 | async-start | bytes 524288 | tf_op jit(solution)/shard_map/all_to_all | solution.py:34
  69.6 3.4 %fusion.59 = f32[64,32,128]{2,0,1:T(8,128)} fusion(f32[64,32,128]{2,1,0:T(8,128)} %get-tuple-element.40), kind=kOutput, calls=%fused_computation.168 | convolution fusion | flops 201330688 | bytes 2097152 | tf_op jit(solution)/shard_map/ij,jyz->iyz/dot_general | solution.py:94
  78.5 2.5 multiply_reduce_fusion.10
  81.0 7.5 %all-reduce.14 = (f32[]{:T(128)}, f32[]{:T(128)}) all-reduce(f32[]{:T(128)} %get-tuple-element.124, f32[]{:T(128)} %multiply_reduce_fusion.10), channel_id=1, replica_groups=mesh['gx_0'=4,'gx_1'=4,'gy_0'=4,'gy_1'=2] {'gx_0'}, use_global_device_ids=true, to_apply=%region_1.2 | all-reduce | flops 2 | bytes 16 | tf_op jit(solution)/shard_map/psum | solution.py:22
  88.5 9.2 %all-reduce.11 = (f32[]{:T(128)}, f32[]{:T(128)}) all-reduce(f32[]{:T(128)} %get-tuple-element.28, f32[]{:T(128)} %get-tuple-element.29), channel_id=1, replica_groups=mesh['gx_0'=4,'gx_1'=4,'gy_0'=4,'gy_1'=2] {'gx_1'}, use_global_device_ids=true, to_apply=%region_2.3 | all-reduce | flops 2 | bytes 16 | tf_op jit(solution)/shard_map/psum | solution.py:22
  97.8 7.7 %all-reduce.8 = (f32[]{:T(128)}, f32[]{:T(128)}) all-reduce(f32[]{:T(128)} %get-tuple-element.19, f32[]{:T(128)} %get-tuple-element.20), channel_id=1, replica_groups=mesh['gx_0'=4,'gx_1'=4,'gy_0'=4,'gy_1'=2] {'gy_0'}, use_global_device_ids=true, to_apply=%region_3.4 | all-reduce | flops 2 | bytes 16 | tf_op jit(solution)/shard_map/psum | solution.py:22
  105.5 9.5 %all-reduce.17 = (f32[]{:T(128)}, f32[]{:T(128)}) all-reduce(f32[]{:T(128)} %get-tuple-element.10, f32[]{:T(128)} %get-tuple-element.11), channel_id=1, replica_groups=mesh['gx_0'=4,'gx_1'=4,'gy_0'=4,'gy_1'=2] {'gy_1'}, use_global_device_ids=true, to_apply=%region_4.5 | all-reduce | flops 2 | bytes 16 | tf_op jit(solution)/shard_map/psum | solution.py:22
  116.4 2.2 multiply_subtract_fusion.29
  118.6 14.6 %maximum_minimum_fusion.2 = (f32[64,32,128]{2,1,0:T(8,128)S(1)}, f32[64,32,128]{2,1,0:T(8,128)}, f32[64,32,128]{2,1,0:T(8,128)}) fusion(f32[64,32,128]{2,1,0:T(8,128)} %param.7, f32[64,32,128]{2,1,0:T(8,128)} %get-tuple-element.125, f32[]{:T(128)S(6)} %mul.590, pred[64,32,128]{2,1,0:T(8,128)(4,1)} %get-tuple-element.99, ...), kind=kLoop, calls=%fused_computation.194 | loop fusion | flops 5242880 | bytes 7340100 | tf_op jit(solution)/shard_map/min | solution.py:193
  136.2 2.2 multiply_reduce_fusion.3
  140.0 3.9 %collective-permute-start.7 = (f32[2,68,2,128]{3,2,1,0:T(2,128)S(1)}, f32[2,68,2,128]{3,2,1,0:T(2,128)S(1)}, u32[]{:S(2)}, u32[]{:S(2)}) collective-permute-start(f32[2,68,2,128]{3,2,1,0:T(2,128)S(1)} %get-tuple-element.83), channel_id=1, source_target_pairs={{0,1},{1,2},{2,3},{3,4},{4,5},{5,6},{6,7},{8,9},{9,10},{10,11},{11... | collective-permute-start | bytes 417800 | tf_op jit(solution)/shard_map/ppermute | solution.py:48
  143.9 1.9 collective-permute-start.6
  149.1 7.0 %all-to-all-start.2 = ((f32[16,1,2,32,128]{4,3,2,1,0:T(8,128)}), f32[16,1,2,32,128]{4,3,2,1,0:T(8,128)}, u32[]{:S(2)}, u32[]{:S(2)}) async-start(f32[16,1,2,32,128]{4,3,2,1,0:T(8,128)} %broadcast_in_dim.121), calls=%async_computation.2 | async-start | bytes 1048576 | tf_op jit(solution)/shard_map/all_to_all | solution.py:34
  166.8 2.2 fusion.20
  171.1 2.2 fusion.35
  173.9 3.9 %multiply_reduce_fusion.9 = (f32[]{:T(128)}, f32[64,32,128]{2,1,0:T(8,128)}) fusion(f32[2,64,32,128]{3,2,1,0:T(8,128)} %fusion.20, f32[64,32,128]{2,1,0:T(8,128)} %get-tuple-element.139), kind=kOutput, calls=%fused_computation.190 | convolution fusion | flops 403718144 | bytes 3145732 | tf_op jit(solution)/shard_map/xyj,jk->xyk/dot_general | solution.py:89
  183.9 9.3 %all-reduce.13 = (f32[]{:T(128)}, f32[]{:T(128)}) all-reduce(f32[]{:T(128)} %get-tuple-element.128, f32[]{:T(128)} %multiply_reduce_fusion.8), channel_id=1, replica_groups=mesh['gx_0'=4,'gx_1'=4,'gy_0'=4,'gy_1'=2] {'gx_0'}, use_global_device_ids=true, to_apply=%region_13.14 | all-reduce | flops 2 | bytes 16 | tf_op jit(solution)/shard_map/psum | solution.py:22
  193.2 9.0 %all-reduce.10 = (f32[]{:T(128)}, f32[]{:T(128)}) all-reduce(f32[]{:T(128)} %get-tuple-element.26, f32[]{:T(128)} %get-tuple-element.27), channel_id=1, replica_groups=mesh['gx_0'=4,'gx_1'=4,'gy_0'=4,'gy_1'=2] {'gx_1'}, use_global_device_ids=true, to_apply=%region_14.15 | all-reduce | flops 2 | bytes 16 | tf_op jit(solution)/shard_map/psum | solution.py:22
  202.2 7.1 %all-reduce.7 = (f32[]{:T(128)}, f32[]{:T(128)}) all-reduce(f32[]{:T(128)} %get-tuple-element.17, f32[]{:T(128)} %get-tuple-element.18), channel_id=1, replica_groups=mesh['gx_0'=4,'gx_1'=4,'gy_0'=4,'gy_1'=2] {'gy_0'}, use_global_device_ids=true, to_apply=%region_15.16 | all-reduce | flops 2 | bytes 16 | tf_op jit(solution)/shard_map/psum | solution.py:22
  209.3 10.8 %all-reduce.16 = (f32[]{:T(128)}, f32[]{:T(128)}) all-reduce(f32[]{:T(128)} %get-tuple-element.8, f32[]{:T(128)} %get-tuple-element.9), channel_id=1, replica_groups=mesh['gx_0'=4,'gx_1'=4,'gy_0'=4,'gy_1'=2] {'gy_1'}, use_global_device_ids=true, to_apply=%region_16.17 | all-reduce | flops 2 | bytes 16 | tf_op jit(solution)/shard_map/psum | solution.py:22
  221.3 2.3 multiply_subtract_fusion.28
  223.6 2.4 maximum_minimum_fusion.1
  228.6 2.2 multiply_reduce_fusion.1
  233.1 3.0 collective-permute-start.11
  236.1 1.9 collective-permute-start.10
  241.6 7.1 %all-to-all-start.3 = ((f32[16,1,2,32,128]{4,3,2,1,0:T(8,128)}), f32[16,1,2,32,128]{4,3,2,1,0:T(8,128)}, u32[]{:S(2)}, u32[]{:S(2)}) async-start(f32[16,1,2,32,128]{4,3,2,1,0:T(8,128)} %broadcast_in_dim.122), calls=%async_computation.3 | async-start | bytes 1048576 | tf_op jit(solution)/shard_map/all_to_all | solution.py:34
  251.9 2.5 fusion.9
  256.4 1.8 multiply_subtract_fusion.1
  260.6 2.2 fusion.17
  266.5 3.8 %multiply_reduce_fusion.7 = (f32[]{:T(128)}, f32[64,32,128]{2,1,0:T(8,128)}) fusion(f32[2,64,32,128]{3,2,1,0:T(8,128)} %fusion.17, f32[64,32,128]{2,1,0:T(8,128)} %get-tuple-element.137), kind=kOutput, calls=%fused_computation.186 | convolution fusion | flops 403718144 | bytes 3145732 | tf_op jit(solution)/shard_map/xyj,jk->xyk/dot_general | solution.py:89
  276.4 2.5 multiply_reduce_fusion.6
  278.9 9.4 %all-reduce.12 = (f32[]{:T(128)}, f32[]{:T(128)}, f32[]{:T(128)}, f32[]{:T(128)}, f32[]{:T(128)}) all-reduce(f32[]{:T(128)} %get-tuple-element.132, f32[]{:T(128)} %multiply_reduce_fusion.6, f32[]{:T(128)S(6)} %div.35, f32[]{:T(128)S(6)} %div.34, f32[]{:T(128)S(6)} %div.33), channel_id=1, replica_groups=mesh['gx_0'=4,'gx_1'=4,'gy_0'=4,'gy_1'=2] {'gx_0'}, use_global_device_ids=true, to_apply=%region_24.25 | all-reduce | flops 5 | bytes 40 | tf_op jit(solution)/shard_map/psum | solution.py:22
  288.3 9.1 %all-reduce.9 = (f32[]{:T(128)}, f32[]{:T(128)}, f32[]{:T(128)}, f32[]{:T(128)}, f32[]{:T(128)}) all-reduce(f32[]{:T(128)} %get-tuple-element.21, f32[]{:T(128)} %get-tuple-element.22, f32[]{:T(128)} %get-tuple-element.23, f32[]{:T(128)} %get-tuple-element.24, ...), channel_id=1, replica_groups=mesh['gx_0'=4,'gx_1'=4,'gy_0'=4,'gy_1'=2] {'gx_1'}, use_global_device_ids=true, to_apply=%region_25.26 | all-reduce | flops 5 | bytes 40 | tf_op jit(solution)/shard_map/psum | solution.py:22
  297.3 7.4 %all-reduce.6 = (f32[]{:T(128)}, f32[]{:T(128)}, f32[]{:T(128)}, f32[]{:T(128)}, f32[]{:T(128)}) all-reduce(f32[]{:T(128)} %get-tuple-element.12, f32[]{:T(128)} %get-tuple-element.13, f32[]{:T(128)} %get-tuple-element.14, f32[]{:T(128)} %get-tuple-element.15, ...), channel_id=1, replica_groups=mesh['gx_0'=4,'gx_1'=4,'gy_0'=4,'gy_1'=2] {'gy_0'}, use_global_device_ids=true, to_apply=%region_26.27 | all-reduce | flops 5 | bytes 40 | tf_op jit(solution)/shard_map/psum | solution.py:22
  304.8 10.5 %all-reduce.15 = (f32[]{:T(128)}, f32[]{:T(128)}, f32[1]{0:T(128)}, f32[1]{0:T(128)}, f32[1]{0:T(128)}) all-reduce(f32[]{:T(128)} %get-tuple-element.3, f32[]{:T(128)} %get-tuple-element.4, f32[1]{0:T(128)} %bitcast.79, f32[1]{0:T(128)} %bitcast.75, f32[1]{0:T(128)} %bitcast.71), channel_id=1, replica_groups=mesh['gx_0'=4,'gx_1'=4,'gy_0'=4,'gy_1'=2] {'gy_1'}, use_global_device_ids=true, to_apply=%region_27.28 | all-reduce | flops 5 | bytes 40 | tf_op jit(solution)/shard_map/psum | solution.py:22
  316.7 3.1 multiply_subtract_fusion.27
  321.2 2.5 pad_maximum_fusion.48
  (160 shorter events, 72.5 us)
Async XLA Ops:
  0.6 6.3 %copy-start = (f32[64,32,128]{2,1,0:T(8,128)S(1)}, f32[64,32,128]{2,1,0:T(8,128)}, u32[]{:S(2)}) copy-start(f32[64,32,128]{2,1,0:T(8,128)} %param.8) | copy-start | bytes 3145732
  0.6 18.1 %copy-start.1 = (f32[64,32,128]{2,1,0:T(8,128)S(1)}, f32[64,32,128]{2,1,0:T(8,128)}, u32[]{:S(2)}) copy-start(f32[64,32,128]{2,1,0:T(8,128)} %param.7) | copy-start | bytes 3145732
  0.7 18.1 %copy-start.6 = (f32[64,32,128]{2,1,0:T(8,128)S(1)}, f32[64,32,128]{2,1,0:T(8,128)}, u32[]{:S(2)}) copy-start(f32[64,32,128]{2,1,0:T(8,128)} %param.9) | copy-start | bytes 3145732
  1.6 22.7 %collective-permute-start = (f32[2,2,32,128]{3,2,1,0:T(8,128)S(1)}, f32[2,2,32,128]{3,2,1,0:T(8,128)S(1)}, u32[]{:S(2)}, u32[]{:S(2)}) collective-permute-start(f32[2,2,32,128]{3,2,1,0:T(8,128)S(1)} %get-tuple-element.91), channel_id=1, source_target_pairs={{0,8},{8,16},{16,24},{24,32},{32,40},{40,48},{48,56},{56,64},{64,7... | collective-permute-start | bytes 196616 | tf_op jit(solution)/shard_map/ppermute | solution.py:48
  5.6 18.8 %collective-permute-start.1 = (f32[2,2,32,128]{3,2,1,0:T(8,128)S(1)}, f32[2,2,32,128]{3,2,1,0:T(8,128)S(1)}, u32[]{:S(2)}, u32[]{:S(2)}) collective-permute-start(f32[2,2,32,128]{3,2,1,0:T(8,128)S(1)} %get-tuple-element.92), channel_id=1, source_target_pairs={{8,0},{16,8},{24,16},{32,24},{40,32},{48,40},{56,48},{64,56},{72,6... | collective-permute-start | bytes 196616 | tf_op jit(solution)/shard_map/ppermute | solution.py:49
  8.2 1.0 copy-start.19
  10.1 45.5 %all-to-all-start = ((f32[16,1,2,32,128]{4,3,2,1,0:T(8,128)}), f32[16,1,2,32,128]{4,3,2,1,0:T(8,128)}, u32[]{:S(2)}, u32[]{:S(2)}) async-start(f32[16,1,2,32,128]{4,3,2,1,0:T(8,128)} %broadcast_in_dim.119), calls=%async_computation | async-start | bytes 1048576 | tf_op jit(solution)/shard_map/all_to_all | solution.py:34
  18.7 3.4 %copy-start.27 = (s32[64,32,128]{2,1,0:T(8,128)S(1)}, s32[64,32,128]{2,1,0:T(8,128)}, u32[]{:S(2)}) copy-start(s32[64,32,128]{2,1,0:T(8,128)} %param.11) | copy-start | bytes 3145732
  22.1 9.4 %copy-start.29 = (f32[8]{0:T(128)S(1)}, f32[8]{0:T(128)}, u32[]{:S(2)}) copy-start(f32[8]{0:T(128)} %param.12) | copy-start | bytes 100
  22.1 10.1 %copy-start.30 = (f32[8]{0:T(128)S(1)}, f32[8]{0:T(128)}, u32[]{:S(2)}) copy-start(f32[8]{0:T(128)} %param.13) | copy-start | bytes 100
  24.5 8.4 %collective-permute-start.3 = (f32[2,68,2,128]{3,2,1,0:T(2,128)S(1)}, f32[2,68,2,128]{3,2,1,0:T(2,128)S(1)}, u32[]{:S(2)}, u32[]{:S(2)}) collective-permute-start(f32[2,68,2,128]{3,2,1,0:T(2,128)S(1)} %get-tuple-element.85), channel_id=1, source_target_pairs={{0,1},{1,2},{2,3},{3,4},{4,5},{5,6},{6,7},{8,9},{9,10},{10,11},{11... | collective-permute-start | bytes 417800 | tf_op jit(solution)/shard_map/ppermute | solution.py:48
  29.1 6.4 %collective-permute-start.2 = (f32[2,68,2,128]{3,2,1,0:T(2,128)S(1)}, f32[2,68,2,128]{3,2,1,0:T(2,128)S(1)}, u32[]{:S(2)}, u32[]{:S(2)}) collective-permute-start(f32[2,68,2,128]{3,2,1,0:T(2,128)S(1)} %get-tuple-element.86), channel_id=1, source_target_pairs={{1,0},{2,1},{3,2},{4,3},{5,4},{6,5},{7,6},{9,8},{10,9},{11,10},{12... | collective-permute-start | bytes 417800 | tf_op jit(solution)/shard_map/ppermute | solution.py:49
  43.2 1.3 copy-start.14
  43.2 1.7 copy-start.17
  47.8 3.7 %copy-start.24 = (f32[64,32,128]{2,0,1:T(8,128)S(1)}, f32[64,32,128]{2,0,1:T(8,128)}, u32[]{:S(2)}) copy-start(f32[64,32,128]{2,0,1:T(8,128)} %get-tuple-element.141) | copy-start | bytes 3145732
  57.0 0.8 copy-start.26
  57.8 20.7 %copy-start.3 = (f32[2,64,32,128]{3,2,1,0:T(8,128)S(1)}, f32[2,64,32,128]{3,2,1,0:T(8,128)}, u32[]{:S(2)}) copy-start(f32[2,64,32,128]{3,2,1,0:T(8,128)} %fusion.23) | copy-start | bytes 6291460
  62.5 14.7 %all-to-all-start.1 = ((f32[16,1,32,128]{3,2,1,0:T(8,128)}), f32[16,1,32,128]{3,2,1,0:T(8,128)}, u32[]{:S(2)}, u32[]{:S(2)}) async-start(f32[16,1,32,128]{3,2,1,0:T(8,128)} %broadcast_in_dim.120), calls=%async_computation.1 | async-start | bytes 524288 | tf_op jit(solution)/shard_map/all_to_all | solution.py:34
  78.5 40.1 %copy-start.28 = (pred[64,32,128]{2,1,0:T(8,128)(4,1)S(1)}, pred[64,32,128]{2,1,0:T(8,128)(4,1)}, u32[]{:S(2)}) copy-start(pred[64,32,128]{2,1,0:T(8,128)(4,1)} %get-tuple-element.93) | copy-start | bytes 786436
  133.2 2.9 copy-start.7
  133.2 5.1 %collective-permute-start.4 = (f32[2,2,32,128]{3,2,1,0:T(8,128)S(1)}, f32[2,2,32,128]{3,2,1,0:T(8,128)S(1)}, u32[]{:S(2)}, u32[]{:S(2)}) collective-permute-start(f32[2,2,32,128]{3,2,1,0:T(8,128)S(1)} %get-tuple-element.89), channel_id=1, source_target_pairs={{0,8},{8,16},{16,24},{24,32},{32,40},{40,48},{48,56},{56,64},{64,7... | collective-permute-start | bytes 196616 | tf_op jit(solution)/shard_map/ppermute | solution.py:48
  134.8 5.0 %collective-permute-start.5 = (f32[2,2,32,128]{3,2,1,0:T(8,128)S(1)}, f32[2,2,32,128]{3,2,1,0:T(8,128)S(1)}, u32[]{:S(2)}, u32[]{:S(2)}) collective-permute-start(f32[2,2,32,128]{3,2,1,0:T(8,128)S(1)} %get-tuple-element.90), channel_id=1, source_target_pairs={{8,0},{16,8},{24,16},{32,24},{40,32},{48,40},{56,48},{64,56},{72,6... | collective-permute-start | bytes 196616 | tf_op jit(solution)/shard_map/ppermute | solution.py:49
  140.0 16.1 %collective-permute-start.7 = (f32[2,68,2,128]{3,2,1,0:T(2,128)S(1)}, f32[2,68,2,128]{3,2,1,0:T(2,128)S(1)}, u32[]{:S(2)}, u32[]{:S(2)}) collective-permute-start(f32[2,68,2,128]{3,2,1,0:T(2,128)S(1)} %get-tuple-element.83), channel_id=1, source_target_pairs={{0,1},{1,2},{2,3},{3,4},{4,5},{5,6},{6,7},{8,9},{9,10},{10,11},{11... | collective-permute-start | bytes 417800 | tf_op jit(solution)/shard_map/ppermute | solution.py:48
  143.9 12.2 %collective-permute-start.6 = (f32[2,68,2,128]{3,2,1,0:T(2,128)S(1)}, f32[2,68,2,128]{3,2,1,0:T(2,128)S(1)}, u32[]{:S(2)}, u32[]{:S(2)}) collective-permute-start(f32[2,68,2,128]{3,2,1,0:T(2,128)S(1)} %get-tuple-element.84), channel_id=1, source_target_pairs={{1,0},{2,1},{3,2},{4,3},{5,4},{6,5},{7,6},{9,8},{10,9},{11,10},{12... | collective-permute-start | bytes 417800 | tf_op jit(solution)/shard_map/ppermute | solution.py:49
  147.1 1.0 copy-start.22
  149.1 28.7 %all-to-all-start.2 = ((f32[16,1,2,32,128]{4,3,2,1,0:T(8,128)}), f32[16,1,2,32,128]{4,3,2,1,0:T(8,128)}, u32[]{:S(2)}, u32[]{:S(2)}) async-start(f32[16,1,2,32,128]{4,3,2,1,0:T(8,128)} %broadcast_in_dim.121), calls=%async_computation.2 | async-start | bytes 1048576 | tf_op jit(solution)/shard_map/all_to_all | solution.py:34
  161.5 1.1 copy-start.2
  164.4 1.3 copy-start.15
  164.4 1.7 copy-start.18
  173.9 6.0 %copy-start.9 = (f32[64,32,128]{2,1,0:T(8,128)S(1)}, f32[64,32,128]{2,1,0:T(8,128)}, u32[]{:S(2)}) copy-start(f32[64,32,128]{2,1,0:T(8,128)} %param.10) | copy-start | bytes 3145732
  177.7 2.2 copy-start.23
  179.9 2.7 copy-start.4
  182.5 1.3 copy-start.5
  223.5 5.1 %copy-start.8 = (f32[64,32,128]{2,1,0:T(8,128)S(1)}, f32[64,32,128]{2,1,0:T(8,128)}, u32[]{:S(2)}) copy-start(f32[64,32,128]{2,1,0:T(8,128)} %param.9) | copy-start | bytes 3145732
  226.0 4.8 %collective-permute-start.8 = (f32[2,2,32,128]{3,2,1,0:T(8,128)S(1)}, f32[2,2,32,128]{3,2,1,0:T(8,128)S(1)}, u32[]{:S(2)}, u32[]{:S(2)}) collective-permute-start(f32[2,2,32,128]{3,2,1,0:T(8,128)S(1)} %get-tuple-element.87), channel_id=1, source_target_pairs={{0,8},{8,16},{16,24},{24,32},{32,40},{40,48},{48,56},{56,64},{64,7... | collective-permute-start | bytes 196616 | tf_op jit(solution)/shard_map/ppermute | solution.py:48
  227.3 5.0 %collective-permute-start.9 = (f32[2,2,32,128]{3,2,1,0:T(8,128)S(1)}, f32[2,2,32,128]{3,2,1,0:T(8,128)S(1)}, u32[]{:S(2)}, u32[]{:S(2)}) collective-permute-start(f32[2,2,32,128]{3,2,1,0:T(8,128)S(1)} %get-tuple-element.88), channel_id=1, source_target_pairs={{8,0},{16,8},{24,16},{32,24},{40,32},{48,40},{56,48},{64,56},{72,6... | collective-permute-start | bytes 196616 | tf_op jit(solution)/shard_map/ppermute | solution.py:49
  233.1 15.6 %collective-permute-start.11 = (f32[2,68,2,128]{3,2,1,0:T(2,128)}, f32[2,68,2,128]{3,2,1,0:T(2,128)S(1)}, u32[]{:S(2)}, u32[]{:S(2)}) collective-permute-start(f32[2,68,2,128]{3,2,1,0:T(2,128)} %get-tuple-element.81), channel_id=1, source_target_pairs={{0,1},{1,2},{2,3},{3,4},{4,5},{5,6},{6,7},{8,9},{9,10},{10,11},{11... | collective-permute-start | bytes 417800 | tf_op jit(solution)/shard_map/ppermute | solution.py:48
  236.1 12.6 %collective-permute-start.10 = (f32[2,68,2,128]{3,2,1,0:T(2,128)}, f32[2,68,2,128]{3,2,1,0:T(2,128)}, u32[]{:S(2)}, u32[]{:S(2)}) collective-permute-start(f32[2,68,2,128]{3,2,1,0:T(2,128)} %get-tuple-element.82), channel_id=1, source_target_pairs={{1,0},{2,1},{3,2},{4,3},{5,4},{6,5},{7,6},{9,8},{10,9},{11,10},{12... | collective-permute-start | bytes 417800 | tf_op jit(solution)/shard_map/ppermute | solution.py:49
  239.4 10.6 %copy-start.20 = (f32[64,32,128]{2,0,1:T(8,128)}, f32[64,32,128]{2,0,1:T(8,128)S(1)}, u32[]{:S(2)}) copy-start(f32[64,32,128]{2,0,1:T(8,128)S(1)} %get-tuple-element.135) | copy-start | bytes 3145732
  241.6 28.8 %all-to-all-start.3 = ((f32[16,1,2,32,128]{4,3,2,1,0:T(8,128)}), f32[16,1,2,32,128]{4,3,2,1,0:T(8,128)}, u32[]{:S(2)}, u32[]{:S(2)}) async-start(f32[16,1,2,32,128]{4,3,2,1,0:T(8,128)} %broadcast_in_dim.122), calls=%async_computation.3 | async-start | bytes 1048576 | tf_op jit(solution)/shard_map/all_to_all | solution.py:34
  258.2 1.3 copy-start.13
  258.2 1.7 copy-start.16
  266.5 6.0 %copy-start.10 = (f32[64,32,128]{2,1,0:T(8,128)S(1)}, f32[64,32,128]{2,1,0:T(8,128)}, u32[]{:S(2)}) copy-start(f32[64,32,128]{2,1,0:T(8,128)} %param.10) | copy-start | bytes 3145732
  270.4 2.2 copy-start.21
  316.7 3.1 copy-start.11
  316.7 3.1 copy-start.12
  316.7 3.1 copy-start.25
where the time goes:
time: 330 us; the launch traced here: 324 us
  blocking collectives  107 us (32%)
  other arithmetic  89.5 us (27%)
  starting transfers between devices  58.2 us (18%)
  matrix products  33.9 us (10%)
  between operations  14.7 us (4%)
  local copies, waits for them, and re-layouts  13.6 us (4%)
  waiting for transfers between devices  7.34 us (2%)
    psum x12, blocking collectives, over_axes(): value = lax.psum(value, axis)  107 us
    all_to_all x4, starting transfers between devices, copy_for_each(): return lax.all_to_all(copies, axis, split_axis=0, concat_axis=0, tiled=True)  29.7 us
    dot_general x6, matrix products, depth_prefix(): jnp.einsum('xyj,jk->xyk', values, table, precision=lax.Precision.HIGHEST)  19.6 us
    min x3, other arithmetic, local(): density_now = jnp.minimum(jnp.maximum(moved, lower_bound), upper_bound)  18.5 us
    ppermute x6, starting transfers between devices, with_halo(): before = lax.ppermute(last, axis, up)  18.4 us
    ppermute x6, starting transfers between devices, with_halo(): after = lax.ppermute(initial, axis, down)  10.1 us
    dot_general x6, matrix products, rows_prefix(): jnp.einsum('ij,jyz->iyz', table, values, precision=lax.Precision.HIGHEST)  9.98 us
    sub x3, other arithmetic, local(): slowness_now - ETA * grad_slowness * lax.rsqrt(norm_slowness / cells + EP...  7.55 us
  transfers between devices with their start and end apart: 16, of which 4 were waited for; matrix products, arithmetic and copies ran while one was open for 24% of the time, Pallas kernels for 0%

commit v1 on v0

v1 whole, which is shorter than its diff:
```python
import functools
import math

import jax
import jax.numpy as jnp
from jax import lax
from jax.experimental import pallas as pl
from jax.experimental.pallas import tpu as pltpu
from jax.sharding import PartitionSpec as P

ITERS = 3
ETA = 0.5
EPSILON = 1e-06
MESH = pl.DeviceIdType.MESH
PAD = 8
RIM = 2


def depth_difference(values):
    lane = lax.broadcasted_iota(jnp.int32, values.shape, values.ndim - 1)
    last = values.shape[-1] - 1
    after = pltpu.roll(values, last, values.ndim - 1)
    before = pltpu.roll(values, 1, values.ndim - 1)
    return jnp.where(lane == last, 0.0, after) - jnp.where(lane == 0, 0.0, before)


def halves(values):
    high = values.astype(jnp.bfloat16)
    low = (values - high.astype(jnp.float32)).astype(jnp.bfloat16)
    return jnp.concatenate([high, low], axis=-1)


def kernel(
    nx,
    ny,
    density,
    slowness,
    pressure,
    times,
    zones,
    low_table,
    high_table,
    density_out,
    slowness_out,
    objective,
    field,
    grads,
    zone,
    lower,
    upper,
    lever,
    fixed,
    linear,
    pobs,
    tobs,
    table,
    rev_table,
    column_send,
    column_recv,
    norm_send,
    norm_recv,
    load_sem,
    rim_send,
    rim_recv,
    zone_send,
    zone_recv,
    col_send_sem,
    col_recv_sem,
    norm_send_sem,
    norm_recv_sem,
    out_sem,
):
    sx, sy, depth = density.shape
    px, py = sx + 2 * RIM, sy + 2 * PAD
    cells = float(nx * sx * ny * sy * depth)
    zscale = 1.0 / math.sqrt(depth)
    xscale = 1.0 / math.sqrt(nx * sx)
    gx, gy = lax.axis_index("gx"), lax.axis_index("gy")
    own_x, own_y = pl.ds(RIM, sx), pl.ds(PAD, sy)

    loads = [
        pltpu.make_async_copy(slowness, field.at[1, own_x, own_y], load_sem.at[0]),
        pltpu.make_async_copy(times, tobs, load_sem.at[1]),
        pltpu.make_async_copy(density, field.at[0, own_x, own_y], load_sem.at[2]),
        pltpu.make_async_copy(zones, zone.at[own_x, own_y], load_sem.at[3]),
        pltpu.make_async_copy(pressure, pobs, load_sem.at[4]),
    ]
    for copy in loads:
        copy.start()

    def turned(value, step, size):
        return lax.rem(value + step, size)

    barrier = pltpu.get_barrier_semaphore()
    greet = [(turned(gx, k, nx), gy) for k in range(1, nx)]
    greet += [(gx, turned(gy, k, ny)) for k in range(1, ny)]
    greet += [(turned(gx, i, nx), turned(gy, j, ny)) for i in (1, nx - 1) for j in (1, ny - 1)]
    for device in greet:
        pl.semaphore_signal(barrier, inc=1, device_id=device, device_id_type=MESH)

    @pl.when(gy == 0)
    def _():
        for buffer in (field, grads):
            buffer[:, :, 0:PAD] = jnp.zeros((buffer.shape[0], px, PAD, depth), jnp.float32)

    @pl.when(gy == ny - 1)
    def _():
        for buffer in (field, grads):
            buffer[:, :, PAD + sy :] = jnp.zeros((buffer.shape[0], px, PAD, depth), jnp.float32)

    @pl.when(gx == 0)
    def _():
        for buffer in (field, grads):
            buffer[:, 0:RIM] = jnp.zeros((buffer.shape[0], RIM, py, depth), jnp.float32)

    @pl.when(gx == nx - 1)
    def _():
        for buffer in (field, grads):
            buffer[:, RIM + sx :] = jnp.zeros((buffer.shape[0], RIM, py, depth), jnp.float32)

    row = lax.broadcasted_iota(jnp.int32, (depth, depth), 0)
    col = lax.broadcasted_iota(jnp.int32, (depth, depth), 1)
    upward = jnp.where(row <= col, 1.0, 0.0).astype(jnp.bfloat16)
    both = (depth - jnp.maximum(row, col)).astype(jnp.float32).astype(jnp.bfloat16)
    downward = jnp.where(row >= col, 1.0, 0.0).astype(jnp.bfloat16)
    for half in range(2):
        rows = pl.ds(half * depth, depth)
        table[rows, pl.ds(0, depth)] = upward
        table[rows, pl.ds(depth, depth)] = both
        rev_table[rows, :] = downward

    pl.semaphore_wait(barrier, len(greet))

    def rim_copies(buffer, lead, send_sems, recv_sems):
        first_x, last_x = pl.ds(RIM, RIM), pl.ds(RIM + sx - RIM, RIM)
        before_x, after_x = pl.ds(0, RIM), pl.ds(RIM + sx, RIM)
        first_y, last_y = pl.ds(PAD, RIM), pl.ds(PAD + sy - RIM, RIM)
        before_y, after_y = pl.ds(PAD - RIM, RIM), pl.ds(PAD + sy, RIM)
        one = lambda at: pl.ds(at, 1)
        up_x, down_x, up_y, down_y = gx < nx - 1, gx > 0, gy < ny - 1, gy > 0
        plans = [
            (up_y, down_y, (0, 1), (own_x, last_y), (own_x, before_y)),
            (down_y, up_y, (0, -1), (own_x, first_y), (own_x, after_y)),
            (up_x, down_x, (1, 0), (last_x, own_y), (before_x, own_y)),
            (down_x, up_x, (-1, 0), (first_x, own_y), (after_x, own_y)),
        ]
        ends_x = {1: (one(RIM + sx - 1), one(RIM - 1)), -1: (one(RIM), one(RIM + sx))}
        ends_y = {1: (one(PAD + sy - 1), one(PAD - 1)), -1: (one(PAD), one(PAD + sy))}
        has_x = {1: (up_x, down_x), -1: (down_x, up_x)}
        has_y = {1: (up_y, down_y), -1: (down_y, up_y)}
        for i in (1, -1):
            for j in (1, -1):
                plans.append(
                    (
                        has_x[i][0] & has_y[j][0],
                        has_x[i][1] & has_y[j][1],
                        (i, j),
                        (ends_x[i][0], ends_y[j][0]),
                        (ends_x[i][1], ends_y[j][1]),
                    )
                )
        copies = []
        for k, (sends, receives, (i, j), source, target) in enumerate(plans):
            copy = pltpu.make_async_remote_copy(
                src_ref=buffer.at[(*lead, *source)],
                dst_ref=buffer.at[(*lead, *target)],
                send_sem=send_sems(k),
                recv_sem=recv_sems(k),
                device_id=(gx + i, gy + j),
                device_id_type=MESH,
            )
            copies.append((sends, receives, copy))
        return copies

    def start_rims(copies):
        for sends, _, copy in copies:
            pl.when(sends)(copy.start)

    def arrived(copies):
        for _, receives, copy in copies:
            pl.when(receives)(copy.wait_recv)

    def sent(copies):
        for sends, _, copy in copies:
            pl.when(sends)(copy.wait_send)

    def start_columns(phase):
        for k in range(1, nx):
            to = turned(gx, k, nx)
            pltpu.make_async_remote_copy(
                src_ref=column_send.at[phase, jnp.where(to > gx, 0, 1)],
                dst_ref=column_recv.at[phase, gx],
                send_sem=col_send_sem.at[phase],
                recv_sem=col_recv_sem.at[phase],
                device_id=(to, gy),
                device_id_type=MESH,
            ).start()

    def columns_arrived(phase):
        rest = column_recv.at[phase, pl.ds(0, nx - 1)]
        pltpu.make_async_copy(rest, rest, col_recv_sem.at[phase]).wait()

    def columns_summed(phase):
        zero = jnp.zeros((sy, depth), jnp.float32)
        earlier, later = zero, zero
        for k in range(nx):
            value = column_recv[phase, k]
            earlier = earlier + jnp.where(gx > k, value, 0.0)
            later = later + jnp.where(gx < k, value, 0.0)
        return earlier, later

    near = [0, 1, 2, 1]
    lane = lax.broadcasted_iota(jnp.int32, (1, depth), 1)
    steps = [(i, j) for i in range(nx) for j in range(ny) if i or j]
    if nx == 16 and ny == 8:
        steps.sort(key=lambda t: -(near[t[0] // 4] + near[t[0] % 4] + near[t[1] // 2]))
    others = nx * ny - 1

    def start_norms(phase, values):
        line = jnp.zeros((1, depth), jnp.float32)
        for k, value in enumerate(values):
            total = jnp.sum(jnp.sum(value, axis=0, keepdims=True), axis=1, keepdims=True)
            line = jnp.where(lane == k, total, line)
        norm_send[phase] = line
        to_x = [turned(gx, i, nx) for i in range(nx)]
        to_y = [turned(gy, j, ny) for j in range(ny)]
        for i, j in steps:
            pltpu.make_async_remote_copy(
                src_ref=norm_send.at[phase],
                dst_ref=norm_recv.at[phase, i * ny + j - 1],
                send_sem=norm_send_sem.at[phase],
                recv_sem=norm_recv_sem.at[phase],
                device_id=(to_x[i], to_y[j]),
                device_id_type=MESH,
            ).start()

    def norms(phase):
        everyone = norm_recv.at[phase]
        pltpu.make_async_copy(everyone, everyone, norm_recv_sem.at[phase]).wait()
        line = jnp.sum(norm_recv[phase], axis=0) + norm_send[phase]
        pick = lambda k: jnp.sum(jnp.where(lane == k, line, 0.0), axis=1, keepdims=True)
        step_density = ETA * lax.rsqrt(pick(0) * (1.0 / cells) + EPSILON)
        step_slowness = ETA * lax.rsqrt(pick(1) * (1.0 / cells) + EPSILON)
        objective[phase] = jnp.sum(jnp.where(lane == 2, line, 0.0)) * (0.5 / cells)
        return step_density, step_slowness

    loads[0].wait()
    loads[1].wait()

    def first_sums(x, carry):
        running, weighted, observed = carry
        running = running + field[1, x + RIM, own_y]
        return running, weighted + running, observed + tobs[x]

    zero = jnp.zeros((sy, depth), jnp.float32)
    total, weighted, observed = lax.fori_loop(0, sx, first_sums, (zero, zero, zero), unroll=4)
    later_parts = (nx - 1 - gx).astype(jnp.float32) * float(sx)
    column_send[0, 0] = total
    column_send[0, 1] = xscale * (weighted + later_parts * total) - observed
    loads[2].wait()
    rims = rim_copies(
        field, (pl.ds(0, 2),), lambda k: rim_send.at[0, k], lambda k: rim_recv.at[0, k]
    )
    start_rims(rims)
    start_columns(0)
    loads[3].wait()
    zone_rims = rim_copies(zone, (), lambda k: zone_send.at[k], lambda k: zone_recv.at[k])
    start_rims(zone_rims)

    loads[4].wait()
    planes = 8

    def fix(step, carry):
        at = pl.multiple_of(step * planes, planes)
        values = pobs[pl.ds(at, planes)].reshape(planes * sy, depth)
        back = jnp.dot(halves(values), rev_table[...], preferred_element_type=jnp.float32)
        fixed[pl.ds(at, planes)] = (back * zscale).reshape(planes, sy, depth)
        return carry

    lax.fori_loop(0, sx // planes, fix, 0)

    def integrate(values, at, squares):
        out = jnp.dot(
            halves(values.reshape(planes * sy, depth)),
            table[...],
            preferred_element_type=jnp.float32,
        )
        miss = out[:, :depth] * zscale - pobs[pl.ds(at, planes)].reshape(planes * sy, depth)
        pull = (out[:, depth:] * (zscale * zscale)).reshape(planes, sy, depth)
        linear[pl.ds(at, planes)] = pull - fixed[pl.ds(at, planes)]
        return squares + jnp.sum((miss * miss).reshape(planes * sy // 8, 8, depth), axis=0)

    zero_tile = jnp.zeros((8, depth), jnp.float32)

    def first_integrals(step, squares):
        at = pl.multiple_of(step * planes, planes)
        return integrate(field[0, pl.ds(at + RIM, planes), own_y], at, squares)

    miss_squares = lax.fori_loop(0, sx // planes, first_integrals, zero_tile)

    def look_up(x, carry):
        number = zone[x]
        low = jnp.zeros(number.shape, jnp.float32)
        high = low
        for k in range(low_table.shape[0]):
            hit = number == k
            low = jnp.where(hit, low_table[k], low)
            high = jnp.where(hit, high_table[k], high)
        lower[x] = low
        upper[x] = high
        return carry

    wide = pl.ds(PAD - 1, sy + 8)

    def levers(p, squares):
        first_vec, second_vec = [], []
        for index, vec in ((0, first_vec), (1, second_vec)):
            vec.append(field[index, p + 1, wide] - field[index, p - 1, wide])
            vec.append(field[index, p, pl.ds(PAD, sy + 8)] - field[index, p, pl.ds(PAD - 2, sy + 8)])
            vec.append(depth_difference(field[index, p, wide]))
        crossed = cross(first_vec, second_vec)
        for index, value in enumerate(cross(second_vec, crossed)):
            lever[index, p, wide] = value
        for index, value in enumerate(cross(crossed, first_vec)):
            lever[3 + index, p, wide] = value
        return squares + (
            crossed[0] * crossed[0] + crossed[1] * crossed[1] + crossed[2] * crossed[2]
        )

    def cross(u, v):
        return (u[1] * v[2] - u[2] * v[1], u[2] * v[0] - u[0] * v[2], u[0] * v[1] - u[1] * v[0])

    def spread(index, p):
        along_x = lever[index, p - 1, own_y] - lever[index, p + 1, own_y]
        along_y = lever[index + 1, p, pl.ds(PAD - 1, sy)] - lever[index + 1, p, pl.ds(PAD + 1, sy)]
        return along_x + along_y - depth_difference(lever[index + 2, p, own_y])

    before = after = None
    rim_sets = [rims]
    for phase in range(ITERS):
        if phase == 0:
            arrived(rims)
        zero_wide = jnp.zeros((sy + 8, depth), jnp.float32)
        crossed_squares = lax.fori_loop(
            RIM, RIM + sx, levers, zero_wide, unroll=2
        )
        levers(RIM - 1, zero_wide)
        levers(RIM + sx, zero_wide)
        wide_row = lax.broadcasted_iota(jnp.int32, zero_wide.shape, 0)
        crossed_squares = jnp.where(
            (wide_row >= 1) & (wide_row < sy + 1), crossed_squares, 0.0
        )
        crossed_squares = jnp.sum(crossed_squares.reshape(-1, 8, depth), axis=0)

        columns_arrived(phase)
        earlier, later = columns_summed(phase)
        if phase == 0:
            before = earlier
            after = (
                later
                + (xscale * later_parts) * (before + total)
                + xscale * (weighted + float(sx) * before)
                - observed
            )
        else:
            after = after - step_slowness * xscale * (
                later
                + later_parts * (earlier + total)
                + weighted
                + float(sx) * earlier
            )
            before = before - step_slowness * earlier

        if phase > 1:
            sent(rim_sets[phase - 1])
        slot = phase % 2

        def descend(x, carry):
            running, ahead, total, weighted, time_squares, squares_d, squares_s = carry
            p = x + RIM
            pull = linear[x] + spread(0, p) * (1.0 / 16.0)
            grads[2 * slot, p, own_y] = pull
            running = running + xscale * field[1, p, own_y]
            miss = running - tobs[x]
            push = xscale * ahead + spread(3, p) * (1.0 / 16.0)
            ahead = ahead - miss
            grads[2 * slot + 1, p, own_y] = push
            total = total + push
            weighted = weighted + total
            return (
                running,
                ahead,
                total,
                weighted,
                time_squares + miss * miss,
                squares_d + pull * pull,
                squares_s + push * push,
            )

        carry = (xscale * before, after, zero, zero, zero, zero, zero)
        _, _, total, weighted, time_squares, squares_d, squares_s = lax.fori_loop(
            0, sx, descend, carry, unroll=2
        )
        tile = lambda v: jnp.sum(v.reshape(sy // 8, 8, depth), axis=0)
        start_norms(
            phase,
            (
                tile(squares_d),
                tile(squares_s),
                tile(time_squares) + miss_squares + crossed_squares * (1.0 / 16.0),
            ),
        )
        if phase < ITERS - 1:
            new_rims = rim_copies(
                grads,
                (pl.ds(2 * slot, 2),),
                lambda k, phase=phase: rim_send.at[phase + 1, k],
                lambda k, phase=phase: rim_recv.at[phase + 1, k],
            )
            rim_sets.append(new_rims)
            start_rims(new_rims)
            column_send[phase + 1, 0] = total
            column_send[phase + 1, 1] = weighted + later_parts * total
            start_columns(phase + 1)
        if phase == 0:
            sent(rims)
            arrived(zone_rims)
            sent(zone_rims)
            lax.fori_loop(0, px, look_up, 0)
        step_density, step_slowness = norms(phase)
        if phase < ITERS - 1:
            arrived(new_rims)

            def move_rim(p, rows):
                d = field[0, p, rows] - step_density * grads[2 * slot, p, rows]
                field[0, p, rows] = jnp.minimum(jnp.maximum(d, lower[p, rows]), upper[p, rows])
                field[1, p, rows] = field[1, p, rows] - step_slowness * grads[2 * slot + 1, p, rows]

            for p in (*range(RIM), *range(RIM + sx, px)):
                move_rim(p, pl.ds(0, py))

            def move(step, squares):
                at = pl.multiple_of(step * planes, planes)
                span = pl.ds(at + RIM, planes)
                d = field[0, span, own_y] - step_density * grads[2 * slot, span, own_y]
                d = jnp.minimum(jnp.maximum(d, lower[span, own_y]), upper[span, own_y])
                field[0, span, own_y] = d
                field[1, span, own_y] = (
                    field[1, span, own_y] - step_slowness * grads[2 * slot + 1, span, own_y]
                )
                for k in range(planes):
                    move_rim(at + RIM + k, pl.ds(0, PAD))
                    move_rim(at + RIM + k, pl.ds(PAD + sy, PAD))
                return integrate(d, at, squares)

            miss_squares = lax.fori_loop(0, sx // planes, move, zero_tile)
        else:

            def finish(x, carry):
                p = x + RIM
                d = field[0, p, own_y] - step_density * grads[2 * slot, p, own_y]
                density_out[x] = jnp.minimum(jnp.maximum(d, lower[p, own_y]), upper[p, own_y])
                slowness_out[x] = field[1, p, own_y] - step_slowness * grads[2 * slot + 1, p, own_y]
                return carry

            lax.fori_loop(0, sx, finish, 0, unroll=2)

    sent(rim_sets[-1])
    for phase in range(ITERS):
        rest = column_recv.at[phase, pl.ds(0, nx - 1)]
        pltpu.make_async_copy(rest, rest, col_send_sem.at[phase]).wait()
        everyone = norm_recv.at[phase]
        pltpu.make_async_copy(everyone, everyone, norm_send_sem.at[phase]).wait()


def solution(mesh):
    nx, ny = mesh.shape["gx"], mesh.shape["gy"]

    def local(density, slowness, pressure, times, zones, low_table, high_table):
        sx, sy, depth = density.shape
        px, py = sx + 2 * RIM, sy + 2 * PAD
        f32, bf16 = jnp.float32, jnp.bfloat16
        hbm = pl.BlockSpec(memory_space=pl.ANY)
        smem = pl.BlockSpec(memory_space=pltpu.SMEM)
        vmem = pl.BlockSpec(memory_space=pltpu.VMEM)
        dma = pltpu.SemaphoreType.DMA
        model = jax.ShapeDtypeStruct((sx, sy, depth), f32)
        return pl.pallas_call(
            functools.partial(kernel, nx, ny),
            out_shape=(model, model, jax.ShapeDtypeStruct((ITERS,), f32)),
            in_specs=[hbm] * 5 + [smem] * 2,
            out_specs=(vmem, vmem, smem),
            scratch_shapes=[
                pltpu.VMEM((2, px, py, depth), f32),
                pltpu.VMEM((4, px, py, depth), f32),
                pltpu.VMEM((px, py, depth), jnp.int32),
                pltpu.VMEM((px, py, depth), f32),
                pltpu.VMEM((px, py, depth), f32),
                pltpu.VMEM((6, px, py, depth), f32),
                pltpu.VMEM((sx, sy, depth), f32),
                pltpu.VMEM((sx, sy, depth), f32),
                pltpu.VMEM((sx, sy, depth), f32),
                pltpu.VMEM((sx, sy, depth), f32),
                pltpu.VMEM((2 * depth, 2 * depth), bf16),
                pltpu.VMEM((2 * depth, depth), bf16),
                pltpu.VMEM((ITERS, 2, sy, depth), f32),
                pltpu.VMEM((ITERS, nx, sy, depth), f32),
                pltpu.VMEM((ITERS, 1, depth), f32),
                pltpu.VMEM((ITERS, nx * ny - 1, 1, depth), f32),
                dma((5,)),
                dma((ITERS, 8)),
                dma((ITERS, 8)),
                dma((8,)),
                dma((8,)),
                dma((ITERS,)),
                dma((ITERS,)),
                dma((ITERS,)),
                dma((ITERS,)),
                dma((2,)),
            ],
            compiler_params=pltpu.CompilerParams(
                collective_id=0,
                has_side_effects=True,
                vmem_limit_bytes=52 * 1024 * 1024,
            ),
        )(density, slowness, pressure, times, zones, low_table, high_table)

    part = P("gx", "gy", None)
    return jax.shard_map(
        local,
        mesh=mesh,
        in_specs=(part,) * 5 + (P(), P()),
        out_specs=(part, part, P()),
        check_vma=False,
    )
```

time: 330 us -> 70.1 us (0.21); the launches traced: 324 us -> 70 us
  blocking collectives: 107 us -> 0 us
  other arithmetic: 89.5 us -> 0 us
  Pallas kernels: 0 us -> 64.9 us
  starting transfers between devices: 58.2 us -> 0 us
  matrix products: 33.9 us -> 0 us
  between operations: 14.7 us -> 0.66 us
  local copies, waits for them, and re-layouts: 13.6 us -> 4.38 us
  waiting for transfers between devices: 7.34 us -> 0 us
    psum x12 -> x0, blocking collectives: 107 us -> none  [over_axes(): value = lax.psum(value, axis)]
    pallas_call x0 -> x1, Pallas kernels: none -> 64.9 us  [local(): pl.pallas_call(functools.partial(kernel, nx, ny), out_shape=(model, model...]
    dot_general x22 -> x0, matrix products: 33.9 us -> none  [the longest x6 19.6 us: depth_prefix(): jnp.einsum('xyj,jk->xyk', values, table, precision=lax.Precision.HIGHEST)]
    all_to_all x4 -> x0, starting transfers between devices: 29.7 us -> none  [copy_for_each(): return lax.all_to_all(copies, axis, split_axis=0, concat_axis=0, tiled=True)]
    ppermute x12 -> x0, starting transfers between devices: 28.5 us -> none  [the longest x6 18.4 us: with_halo(): before = lax.ppermute(last, axis, up)]
    reduce_sum x12 -> x0, other arithmetic: 19.6 us -> none  [the longest x3 6.54 us: local(): jnp.sum(time_miss * time_miss)]
    sub x15 -> x0, other arithmetic: 19 us -> none  [the longest x3 7.55 us: local(): slowness_now - ETA * grad_slowness * lax.rsqrt(norm_slowness / cells + EP...]
    min x3 -> x0, other arithmetic: 18.5 us -> none  [local(): density_now = jnp.minimum(jnp.maximum(moved, lower_bound), upper_bound)]
  transfers between devices with their start and end apart: 16 -> 0, of which waited for: 4 -> 0; matrix products, arithmetic and copies ran while one was open for 24% -> 0% of each run, Pallas kernels for 0% -> 0%
where the time goes in v1:
time: 70.1 us; the launch traced here: 70 us
  Pallas kernels  64.9 us (93%)
  local copies, waits for them, and re-layouts  4.38 us (6%)
    pallas_call x1, Pallas kernels, local(): pl.pallas_call(functools.partial(kernel, nx, ny), out_shape=(model, model...  64.9 us
    unnamed x9, local copies, waits for them, and re-layouts  4.38 us

profile of v1, /device:TPU:1, one launch (start us, length us, event | category | flops | bytes accessed | tf_op | source)
XLA Modules:
  0.0 70.0 jit_solution(9744883348572121850)
XLA Ops:
  0.6 0.0 copy-start
  0.6 0.6 copy-done
  1.3 0.0 copy-start.1
  1.3 0.7 copy-done.1
  1.9 64.9 %shard_map.94 = (f32[64,32,128]{2,1,0:T(8,128)S(1)}, f32[64,32,128]{2,1,0:T(8,128)}, f32[3]{0:T(128)S(1)}) custom-call(f32[64,32,128]{2,1,0:T(8,128)} %density.1, f32[64,32,128]{2,1,0:T(8,128)} %slowness.1, f32[64,32,128]{2,1,0:T(8,128)} %pressure.1, f32[64,32,128]{2,1,0:T(8,128)} %times.1, s32[64,32,128]{2,1,0:T(8,128)} %zones.1, f32[8]{0:T(128)S(1)} %copy-done, ...), custom_call_target="tpu_custom_call" | custom-call | tf_op jit(solution)/shard_map/pallas_call | solution.py:488
  66.9 0.0 copy-start.2
  66.9 1.0 %copy.13 = f32[64,32,128]{2,1,0:T(8,128)} copy(f32[64,32,128]{2,1,0:T(8,128)S(1)} %get-tuple-element.6) | data formatting | bytes 2097152
  67.9 0.6 copy-done.2
  68.5 1.0 %copy.14 = f32[64,32,128]{2,1,0:T(8,128)} copy(f32[64,32,128]{2,1,0:T(8,128)S(1)} %copy-done.2) | data formatting | bytes 2097152
  69.5 0.5 copy.15
Async XLA Ops:
  0.6 0.7 copy-start
  1.3 0.7 copy-start.1
  66.9 1.6 %copy-start.2 = (f32[64,32,128]{2,1,0:T(8,128)S(1)}, f32[64,32,128]{2,1,0:T(8,128)}, u32[]{:S(2)}) copy-start(f32[64,32,128]{2,1,0:T(8,128)} %get-tuple-element.7) | copy-start | bytes 3145732

commit v2 on v1

--- a/solution.py
+++ b/solution.py
@@ -14,6 +14,8 @@
 MESH = pl.DeviceIdType.MESH
 PAD = 8
 RIM = 2
+WHOLE = 16.0
+BATCH = 4
 
 
 def depth_difference(values):
@@ -38,8 +40,8 @@
     pressure,
     times,
     zones,
-    low_table,
-    high_table,
+    lows,
+    highs,
     density_out,
     slowness_out,
     objective,
@@ -49,12 +51,19 @@
     lower,
     upper,
     lever,
+    twist,
+    slope,
+    turn,
+    cums,
+    pulls,
     fixed,
-    linear,
     pobs,
     tobs,
+    lhs,
     table,
     rev_table,
+    low_table,
+    high_table,
     column_send,
     column_recv,
     norm_send,
@@ -68,7 +77,7 @@
     col_recv_sem,
     norm_send_sem,
     norm_recv_sem,
-    out_sem,
+    state,
 ):
     sx, sy, depth = density.shape
     px, py = sx + 2 * RIM, sy + 2 * PAD
@@ -84,6 +93,8 @@
         pltpu.make_async_copy(density, field.at[0, own_x, own_y], load_sem.at[2]),
         pltpu.make_async_copy(zones, zone.at[own_x, own_y], load_sem.at[3]),
         pltpu.make_async_copy(pressure, pobs, load_sem.at[4]),
+        pltpu.make_async_copy(lows, low_table, load_sem.at[5]),
+        pltpu.make_async_copy(highs, high_table, load_sem.at[6]),
     ]
     for copy in loads:
         copy.start()
@@ -121,13 +132,15 @@
     row = lax.broadcasted_iota(jnp.int32, (depth, depth), 0)
     col = lax.broadcasted_iota(jnp.int32, (depth, depth), 1)
     upward = jnp.where(row <= col, 1.0, 0.0).astype(jnp.bfloat16)
-    both = (depth - jnp.maximum(row, col)).astype(jnp.float32).astype(jnp.bfloat16)
+    both = ((depth - jnp.maximum(row, col)).astype(jnp.float32) * (WHOLE / depth)).astype(jnp.bfloat16)
+    differ = (jnp.where(row == col + 1, 1.0, 0.0) - jnp.where(row == col - 1, 1.0, 0.0)).astype(jnp.bfloat16)
     downward = jnp.where(row >= col, 1.0, 0.0).astype(jnp.bfloat16)
     for half in range(2):
-        rows = pl.ds(half * depth, depth)
-        table[rows, pl.ds(0, depth)] = upward
-        table[rows, pl.ds(depth, depth)] = both
-        rev_table[rows, :] = downward
+        tall = pl.ds(half * depth, depth)
+        table[tall, pl.ds(0, depth)] = upward
+        table[tall, pl.ds(depth, depth)] = both
+        table[tall, pl.ds(2 * depth, depth)] = differ
+        rev_table[tall, :] = downward
 
     pl.semaphore_wait(barrier, len(greet))
 
@@ -239,8 +252,9 @@
         pltpu.make_async_copy(everyone, everyone, norm_recv_sem.at[phase]).wait()
         line = jnp.sum(norm_recv[phase], axis=0) + norm_send[phase]
         pick = lambda k: jnp.sum(jnp.where(lane == k, line, 0.0), axis=1, keepdims=True)
-        step_density = ETA * lax.rsqrt(pick(0) * (1.0 / cells) + EPSILON)
-        step_slowness = ETA * lax.rsqrt(pick(1) * (1.0 / cells) + EPSILON)
+        scale = 1.0 / (WHOLE * WHOLE * cells)
+        step_density = (ETA / WHOLE) * lax.rsqrt(pick(0) * scale + EPSILON)
+        step_slowness = (ETA / WHOLE) * lax.rsqrt(pick(1) * scale + EPSILON)
         objective[phase] = jnp.sum(jnp.where(lane == 2, line, 0.0)) * (0.5 / cells)
         return step_density, step_slowness
 
@@ -250,18 +264,20 @@
     def first_sums(x, carry):
         running, weighted, observed = carry
         running = running + field[1, x + RIM, own_y]
-        return running, weighted + running, observed + tobs[x]
+        seen = tobs[x]
+        tobs[x] = seen * (1.0 / xscale)
+        return running, weighted + running, observed + seen
 
     zero = jnp.zeros((sy, depth), jnp.float32)
-    total, weighted, observed = lax.fori_loop(0, sx, first_sums, (zero, zero, zero), unroll=4)
-    later_parts = (nx - 1 - gx).astype(jnp.float32) * float(sx)
-    column_send[0, 0] = total
-    column_send[0, 1] = xscale * (weighted + later_parts * total) - observed
     loads[2].wait()
     rims = rim_copies(
         field, (pl.ds(0, 2),), lambda k: rim_send.at[0, k], lambda k: rim_recv.at[0, k]
     )
     start_rims(rims)
+    total, weighted, observed = lax.fori_loop(0, sx, first_sums, (zero, zero, zero), unroll=4)
+    later_parts = (nx - 1 - gx).astype(jnp.float32) * float(sx)
+    column_send[0, 0] = total
+    column_send[0, 1] = xscale * (weighted + later_parts * total) - observed
     start_columns(0)
     loads[3].wait()
     zone_rims = rim_copies(zone, (), lambda k: zone_send.at[k], lambda k: zone_recv.at[k])
@@ -269,34 +285,50 @@
 
     loads[4].wait()
     planes = 8
+    tall = planes * sy
 
     def fix(step, carry):
-        at = pl.multiple_of(step * planes, planes)
-        values = pobs[pl.ds(at, planes)].reshape(planes * sy, depth)
+        span = pl.ds(pl.multiple_of(step * planes, planes), planes)
+        values = pobs[span].reshape(tall, depth)
         back = jnp.dot(halves(values), rev_table[...], preferred_element_type=jnp.float32)
-        fixed[pl.ds(at, planes)] = (back * zscale).reshape(planes, sy, depth)
+        fixed[span] = (back * (WHOLE * zscale)).reshape(planes, sy, depth)
+        pobs[span] = (values * (1.0 / zscale)).reshape(planes, sy, depth)
         return carry
 
-    lax.fori_loop(0, sx // planes, fix, 0)
-
-    def integrate(values, at, squares):
-        out = jnp.dot(
-            halves(values.reshape(planes * sy, depth)),
-            table[...],
-            preferred_element_type=jnp.float32,
-        )
-        miss = out[:, :depth] * zscale - pobs[pl.ds(at, planes)].reshape(planes * sy, depth)
-        pull = (out[:, depth:] * (zscale * zscale)).reshape(planes, sy, depth)
-        linear[pl.ds(at, planes)] = pull - fixed[pl.ds(at, planes)]
-        return squares + jnp.sum((miss * miss).reshape(planes * sy // 8, 8, depth), axis=0)
-
-    zero_tile = jnp.zeros((8, depth), jnp.float32)
-
-    def first_integrals(step, squares):
-        at = pl.multiple_of(step * planes, planes)
-        return integrate(field[0, pl.ds(at + RIM, planes), own_y], at, squares)
-
-    miss_squares = lax.fori_loop(0, sx // planes, first_integrals, zero_tile)
+    lax.fori_loop(0, sx // planes, fix, 0, unroll=2)
+
+    def integrate(step):
+        span = pl.ds(pl.multiple_of(step * planes, planes), planes)
+        flat = pl.ds(pl.multiple_of(step * tall, tall), tall)
+        out = jnp.dot(lhs[flat], table[...], preferred_element_type=jnp.float32)
+        for buffer, k in ((cums, 0), (pulls, 1), (slope.at[0], 2)):
+            buffer[span] = out[:, k * depth : (k + 1) * depth].reshape(planes, sy, depth)
+
+    def in_steps(prepare):
+        prepare(0)
+
+        def body(step, carry):
+            integrate(step - 1)
+            prepare(step)
+            return carry
+
+        lax.fori_loop(1, sx // planes, body, 0)
+        integrate(sx // planes - 1)
+
+    def fill(step, values):
+        lhs[pl.ds(pl.multiple_of(step * tall, tall), tall)] = halves(values.reshape(tall, depth))
+
+    in_steps(lambda k: fill(k, field[0, pl.ds(pl.multiple_of(k * planes, planes) + RIM, planes), own_y]))
+
+    def all_slopes(source, target):
+        def body(step, carry):
+            at = pl.multiple_of(step * planes, planes)
+            target[pl.ds(at, planes)] = depth_difference(source[pl.ds(at + RIM, planes), own_y])
+            return carry
+
+        lax.fori_loop(0, sx // planes, body, 0)
+
+    all_slopes(field.at[1], slope.at[1])
 
     def look_up(x, carry):
         number = zone[x]
@@ -310,64 +342,119 @@
         upper[x] = high
         return carry
 
-    wide = pl.ds(PAD - 1, sy + 8)
-
-    def levers(p, squares):
-        first_vec, second_vec = [], []
-        for index, vec in ((0, first_vec), (1, second_vec)):
-            vec.append(field[index, p + 1, wide] - field[index, p - 1, wide])
-            vec.append(field[index, p, pl.ds(PAD, sy + 8)] - field[index, p, pl.ds(PAD - 2, sy + 8)])
-            vec.append(depth_difference(field[index, p, wide]))
+    groups = sy // 8
+    zero_tile = jnp.zeros((8, depth), jnp.float32)
+    none = (zero_tile,) * groups
+
+    def rows(j):
+        return pl.ds(PAD + j, 8, stride=groups)
+
+    def own(j):
+        return pl.ds(j, 8, stride=groups)
+
+    def tree(values):
+        values = list(values)
+        while len(values) > 1:
+            values = [sum(values[k : k + 2]) for k in range(0, len(values), 2)]
+        return values[0]
+
+    ring = pl.ds(PAD - 1, 2, stride=sy + 1)
+    ring_after = pl.ds(PAD, 2, stride=sy + 1)
+    ring_before = pl.ds(PAD - 2, 2, stride=sy + 1)
+
+    def edge_levers(p):
+        for j in range(groups):
+            first_vec, second_vec = [
+                (
+                    field[f, p + 1, rows(j)] - field[f, p - 1, rows(j)],
+                    field[f, p, rows(j + 1)] - field[f, p, rows(j - 1)],
+                    depth_difference(field[f, p, rows(j)]),
+                )
+                for f in range(2)
+            ]
+            crossed = cross(first_vec, second_vec)
+            lever[0, p, rows(j)] = cross(second_vec, crossed)[0]
+            lever[2, p, rows(j)] = cross(crossed, first_vec)[0]
+
+    def plane_levers(x):
+        p = x + RIM
+        center = [[field[f, p, rows(j)] for j in range(-1, groups + 1)] for f in range(2)]
+        squares = []
+        for j in range(groups):
+            first_vec, second_vec = [
+                (
+                    field[f, p + 1, rows(j)] - field[f, p - 1, rows(j)],
+                    center[f][j + 2] - center[f][j],
+                    slope[f, x, own(j)],
+                )
+                for f in range(2)
+            ]
+            crossed = cross(first_vec, second_vec)
+            for f, vec in ((0, cross(second_vec, crossed)), (1, cross(crossed, first_vec))):
+                lever[2 * f, p, rows(j)] = vec[0]
+                lever[2 * f + 1, p, rows(j)] = vec[1]
+                twist[f, x + BATCH, own(j)] = vec[2]
+            squares.append(tree([c * c for c in crossed]))
+        first_vec, second_vec = [
+            (
+                field[f, p + 1, ring] - field[f, p - 1, ring],
+                field[f, p, ring_after] - field[f, p, ring_before],
+                depth_difference(field[f, p, ring]),
+            )
+            for f in range(2)
+        ]
         crossed = cross(first_vec, second_vec)
-        for index, value in enumerate(cross(second_vec, crossed)):
-            lever[index, p, wide] = value
-        for index, value in enumerate(cross(crossed, first_vec)):
-            lever[3 + index, p, wide] = value
-        return squares + (
-            crossed[0] * crossed[0] + crossed[1] * crossed[1] + crossed[2] * crossed[2]
-        )
+        lever[1, p, ring] = cross(second_vec, crossed)[1]
+        lever[3, p, ring] = cross(crossed, first_vec)[1]
+        return tree(squares)
+
+    def untwist(at):
+        for f in range(2):
+            for k in range(BATCH):
+                for j in range(groups):
+                    twist[f, at + k, own(j)] = depth_difference(twist[f, at + k, own(j)])
+
+    def levers(step, squares):
+        x = step * BATCH
+        untwist(x)
+        return squares + tree([plane_levers(x + k) for k in range(BATCH)])
 
     def cross(u, v):
         return (u[1] * v[2] - u[2] * v[1], u[2] * v[0] - u[0] * v[2], u[0] * v[1] - u[1] * v[0])
 
-    def spread(index, p):
-        along_x = lever[index, p - 1, own_y] - lever[index, p + 1, own_y]
-        along_y = lever[index + 1, p, pl.ds(PAD - 1, sy)] - lever[index + 1, p, pl.ds(PAD + 1, sy)]
-        return along_x + along_y - depth_difference(lever[index + 2, p, own_y])
-
-    before = after = None
+    def spread(f, x):
+        p = x + RIM
+        along = [lever[2 * f + 1, p, rows(j)] for j in range(-1, groups + 1)]
+        return [
+            (lever[2 * f, p - 1, rows(j)] - lever[2 * f, p + 1, rows(j)])
+            + ((along[j] - along[j + 2]) - twist[f, x + BATCH, own(j)])
+            for j in range(groups)
+        ]
+
+    before = ahead = None
     rim_sets = [rims]
     for phase in range(ITERS):
         if phase == 0:
             arrived(rims)
-        zero_wide = jnp.zeros((sy + 8, depth), jnp.float32)
-        crossed_squares = lax.fori_loop(
-            RIM, RIM + sx, levers, zero_wide, unroll=2
-        )
-        levers(RIM - 1, zero_wide)
-        levers(RIM + sx, zero_wide)
-        wide_row = lax.broadcasted_iota(jnp.int32, zero_wide.shape, 0)
-        crossed_squares = jnp.where(
-            (wide_row >= 1) & (wide_row < sy + 1), crossed_squares, 0.0
-        )
-        crossed_squares = jnp.sum(crossed_squares.reshape(-1, 8, depth), axis=0)
+        none = (zero_tile,) * groups
+        crossed_squares = lax.fori_loop(0, sx // BATCH, levers, zero_tile)
+        untwist(sx)
+        edge_levers(RIM - 1)
+        edge_levers(RIM + sx)
 
         columns_arrived(phase)
         earlier, later = columns_summed(phase)
         if phase == 0:
             before = earlier
-            after = (
-                later
-                + (xscale * later_parts) * (before + total)
-                + xscale * (weighted + float(sx) * before)
-                - observed
+            ahead = (
+                later * (1.0 / xscale)
+                + later_parts * (before + total)
+                + (weighted + float(sx) * before)
+                - observed * (1.0 / xscale)
             )
         else:
-            after = after - step_slowness * xscale * (
-                later
-                + later_parts * (earlier + total)
-                + weighted
-                + float(sx) * earlier
+            ahead = ahead - step_slowness * (
+                later + later_parts * (earlier + total) + weighted + float(sx) * earlier
             )
             before = before - step_slowness * earlier
 
@@ -375,39 +462,48 @@
             sent(rim_sets[phase - 1])
         slot = phase % 2
 
-        def descend(x, carry):
-            running, ahead, total, weighted, time_squares, squares_d, squares_s = carry
-            p = x + RIM
-            pull = linear[x] + spread(0, p) * (1.0 / 16.0)
-            grads[2 * slot, p, own_y] = pull
-            running = running + xscale * field[1, p, own_y]
-            miss = running - tobs[x]
-            push = xscale * ahead + spread(3, p) * (1.0 / 16.0)
-            ahead = ahead - miss
-            grads[2 * slot + 1, p, own_y] = push
-            total = total + push
-            weighted = weighted + total
-            return (
-                running,
-                ahead,
-                total,
-                weighted,
-                time_squares + miss * miss,
-                squares_d + pull * pull,
-                squares_s + push * push,
-            )
-
-        carry = (xscale * before, after, zero, zero, zero, zero, zero)
-        _, _, total, weighted, time_squares, squares_d, squares_s = lax.fori_loop(
-            0, sx, descend, carry, unroll=2
-        )
-        tile = lambda v: jnp.sum(v.reshape(sy // 8, 8, depth), axis=0)
+        push_scale = WHOLE * xscale * xscale
+
+        def descend(step, carry):
+            running, push_sum, total, weighted, squares = map(list, carry)
+            for k in range(BATCH):
+                x = step * BATCH + k
+                p = x + RIM
+                spreads = spread(0, x), spread(1, x)
+                terms = [[], [], [], []]
+                for j in range(groups):
+                    fit = cums[x, own(j)] - pobs[x, own(j)]
+                    pull = (pulls[x, own(j)] - fixed[x, own(j)]) + spreads[0][j]
+                    grads[2 * slot, p, rows(j)] = pull
+                    running[j] = running[j] + field[1, p, rows(j)]
+                    miss = running[j] - tobs[x, own(j)]
+                    push = push_scale * push_sum[j] + spreads[1][j]
+                    push_sum[j] = push_sum[j] - miss
+                    grads[2 * slot + 1, p, rows(j)] = push
+                    total[j] = total[j] + push
+                    weighted[j] = weighted[j] + total[j]
+                    for term, value in zip(terms, (pull, push, fit, miss)):
+                        term.append(value * value)
+                squares = [square + tree(term) for square, term in zip(squares, terms)]
+            return tuple(map(tuple, (running, push_sum, total, weighted, squares)))
+
+        state[0] = before
+        state[1] = ahead
+        split = lambda k: tuple(state[k, own(j)] for j in range(groups))
+        carry = (split(0), split(1), none, none, (zero_tile,) * 4)
+        _, _, totals, weights, squares = lax.fori_loop(0, sx // BATCH, descend, carry)
+        for j in range(groups):
+            state[0, own(j)] = totals[j]
+            state[1, own(j)] = weights[j]
+        total, weighted = state[0], state[1]
         start_norms(
             phase,
             (
-                tile(squares_d),
-                tile(squares_s),
-                tile(time_squares) + miss_squares + crossed_squares * (1.0 / 16.0),
+                squares[0],
+                squares[1],
+                squares[2] * (zscale * zscale)
+                + squares[3] * (xscale * xscale)
+                + crossed_squares * (1.0 / 16.0),
             ),
         )
         if phase < ITERS - 1:
@@ -426,34 +522,41 @@
             sent(rims)
             arrived(zone_rims)
             sent(zone_rims)
+            loads[5].wait()
+            loads[6].wait()
             lax.fori_loop(0, px, look_up, 0)
+        if phase < ITERS - 1:
+            all_slopes(grads.at[2 * slot + 1], turn)
         step_density, step_slowness = norms(phase)
         if phase < ITERS - 1:
             arrived(new_rims)
 
-            def move_rim(p, rows):
-                d = field[0, p, rows] - step_density * grads[2 * slot, p, rows]
-                field[0, p, rows] = jnp.minimum(jnp.maximum(d, lower[p, rows]), upper[p, rows])
-                field[1, p, rows] = field[1, p, rows] - step_slowness * grads[2 * slot + 1, p, rows]
+            def move_rim(p, at):
+                d = field[0, p, at] - step_density * grads[2 * slot, p, at]
+                field[0, p, at] = jnp.minimum(jnp.maximum(d, lower[p, at]), upper[p, at])
+                field[1, p, at] = field[1, p, at] - step_slowness * grads[2 * slot + 1, p, at]
 
             for p in (*range(RIM), *range(RIM + sx, px)):
                 move_rim(p, pl.ds(0, py))
 
-            def move(step, squares):
+            def move(step):
                 at = pl.multiple_of(step * planes, planes)
                 span = pl.ds(at + RIM, planes)
                 d = field[0, span, own_y] - step_density * grads[2 * slot, span, own_y]
                 d = jnp.minimum(jnp.maximum(d, lower[span, own_y]), upper[span, own_y])
                 field[0, span, own_y] = d
+                fill(step, d)
                 field[1, span, own_y] = (
                     field[1, span, own_y] - step_slowness * grads[2 * slot + 1, span, own_y]
+                )
+                slope[1, pl.ds(at, planes)] = (
+                    slope[1, pl.ds(at, planes)] - step_slowness * turn[pl.ds(at, planes)]
                 )
                 for k in range(planes):
                     move_rim(at + RIM + k, pl.ds(0, PAD))
                     move_rim(at + RIM + k, pl.ds(PAD + sy, PAD))
-                return integrate(d, at, squares)
-
-            miss_squares = lax.fori_loop(0, sx // planes, move, zero_tile)
+
+            in_steps(move)
         else:
 
             def finish(x, carry):
@@ -478,9 +581,10 @@
 
     def local(density, slowness, pressure, times, zones, low_table, high_table):
         sx, sy, depth = density.shape
+        zones_shape = low_table.shape
         px, py = sx + 2 * RIM, sy + 2 * PAD
         f32, bf16 = jnp.float32, jnp.bfloat16
-        hbm = pl.BlockSpec(memory_space=pl.ANY)
+        hbm = pl.BlockSpec(memory_space=pltpu.HBM)
         smem = pl.BlockSpec(memory_space=pltpu.SMEM)
         vmem = pl.BlockSpec(memory_space=pltpu.VMEM)
         dma = pltpu.SemaphoreType.DMA
@@ -488,7 +592,7 @@
         return pl.pallas_call(
             functools.partial(kernel, nx, ny),
             out_shape=(model, model, jax.ShapeDtypeStruct((ITERS,), f32)),
-            in_specs=[hbm] * 5 + [smem] * 2,
+            in_specs=[hbm] * 7,
             out_specs=(vmem, vmem, smem),
             scratch_shapes=[
                 pltpu.VMEM((2, px, py, depth), f32),
@@ -496,18 +600,20 @@
                 pltpu.VMEM((px, py, depth), jnp.int32),
                 pltpu.VMEM((px, py, depth), f32),
                 pltpu.VMEM((px, py, depth), f32),
-                pltpu.VMEM((6, px, py, depth), f32),
-                pltpu.VMEM((sx, sy, depth), f32),
-                pltpu.VMEM((sx, sy, depth), f32),
-                pltpu.VMEM((sx, sy, depth), f32),
-                pltpu.VMEM((sx, sy, depth), f32),
-                pltpu.VMEM((2 * depth, 2 * depth), bf16),
+                pltpu.VMEM((4, px, py, depth), f32),
+                pltpu.VMEM((2, sx + BATCH, sy, depth), f32),
+                pltpu.VMEM((2, sx, sy, depth), f32),
+                *[pltpu.VMEM((sx, sy, depth), f32)] * 6,
+                pltpu.VMEM((sx * sy, 2 * depth), bf16),
+                pltpu.VMEM((2 * depth, 3 * depth), bf16),
                 pltpu.VMEM((2 * depth, depth), bf16),
+                pltpu.SMEM(zones_shape, f32),
+                pltpu.SMEM(zones_shape, f32),
                 pltpu.VMEM((ITERS, 2, sy, depth), f32),
                 pltpu.VMEM((ITERS, nx, sy, depth), f32),
                 pltpu.VMEM((ITERS, 1, depth), f32),
                 pltpu.VMEM((ITERS, nx * ny - 1, 1, depth), f32),
-                dma((5,)),
+                dma((7,)),
                 dma((ITERS, 8)),
                 dma((ITERS, 8)),
                 dma((8,)),
@@ -516,12 +622,12 @@
                 dma((ITERS,)),
                 dma((ITERS,)),
                 dma((ITERS,)),
-                dma((2,)),
+                pltpu.VMEM((2, sy, depth), f32),
             ],
             compiler_params=pltpu.CompilerParams(
                 collective_id=0,
                 has_side_effects=True,
-                vmem_limit_bytes=52 * 1024 * 1024,
+                vmem_limit_bytes=54 * 1024 * 1024,
             ),
         )(density, slowness, pressure, times, zones, low_table, high_table)
 

time: 70.1 us -> 59.2 us (0.84)
  Pallas kernels: 64.9 us -> 54.6 us
    pallas_call x1, Pallas kernels: 64.9 us -> 54.6 us  [local(): pl.pallas_call(functools.partial(kernel, nx, ny), out_shape=(model, model...]
    unnamed x9 -> x7, local copies, waits for them, and re-layouts: 4.38 us -> 3.84 us
where the time goes in v2:
time: 59.2 us; the launch traced here: 59 us
  Pallas kernels  54.6 us (92%)
  local copies, waits for them, and re-layouts  3.84 us (6%)
  between operations  0.65 us (1%)
    pallas_call x1, Pallas kernels, local(): pl.pallas_call(functools.partial(kernel, nx, ny), out_shape=(model, model...  54.6 us
    unnamed x7, local copies, waits for them, and re-layouts  3.84 us

profile of v2, /device:TPU:1, one launch (start us, length us, event | category | flops | bytes accessed | tf_op | source)
XLA Modules:
  0.0 59.0 jit_solution(16520910191717351123)
XLA Ops:
  0.6 54.6 %shard_map.94 = (f32[64,32,128]{2,1,0:T(8,128)}, f32[64,32,128]{2,1,0:T(8,128)}, f32[3]{0:T(128)}) custom-call(f32[64,32,128]{2,1,0:T(8,128)} %density.1, f32[64,32,128]{2,1,0:T(8,128)} %slowness.1, f32[64,32,128]{2,1,0:T(8,128)} %pressure.1, f32[64,32,128]{2,1,0:T(8,128)} %times.1, s32[64,32,128]{2,1,0:T(8,128)} %zones.1, f32[8]{0:T(128)} %lows.1, f32[8]{0:T(128)} %highs.1), custom_call_target="tpu_custom_call" | custom-call | tf_op jit(solution)/shard_map/pallas_call | solution.py:592
  55.2 0.0 copy-start
  55.2 2.4 %copy.13 = f32[64,32,128]{2,1,0:T(8,128)} copy(f32[64,32,128]{2,1,0:T(8,128)} %get-tuple-element.6) | data formatting | bytes 2097152
  57.6 0.0 copy-done
  57.6 0.0 copy-start.1
  57.6 1.0 %copy.14 = f32[64,32,128]{2,1,0:T(8,128)} copy(f32[64,32,128]{2,1,0:T(8,128)S(1)} %copy-done) | data formatting | bytes 2097152
  58.5 0.0 copy-done.1
  58.5 0.5 copy.15
Async XLA Ops:
  55.2 2.4 %copy-start = (f32[64,32,128]{2,1,0:T(8,128)S(1)}, f32[64,32,128]{2,1,0:T(8,128)}, u32[]{:S(2)}) copy-start(f32[64,32,128]{2,1,0:T(8,128)} %get-tuple-element.7) | copy-start | bytes 3145732
  57.6 1.0 %copy-start.1 = (f32[3]{0:T(128)S(1)}, f32[3]{0:T(128)}, u32[]{:S(2)}) copy-start(f32[3]{0:T(128)} %get-tuple-element.8) | copy-start | bytes 40

commit v3 on v2

--- a/solution.py
+++ b/solution.py
@@ -14,6 +14,7 @@
 MESH = pl.DeviceIdType.MESH
 PAD = 8
 RIM = 2
+LONG = 32
 WHOLE = 16.0
 BATCH = 4
 
@@ -30,6 +31,59 @@
     high = values.astype(jnp.bfloat16)
     low = (values - high.astype(jnp.float32)).astype(jnp.bfloat16)
     return jnp.concatenate([high, low], axis=-1)
+
+
+def steps_of(line, cells):
+    lane = lax.broadcasted_iota(jnp.int32, line.shape, 1)
+    scale = 1.0 / (WHOLE * WHOLE * cells)
+    norm = lambda k: jnp.sum(jnp.where(lane == k, line, 0.0), axis=1, keepdims=True) * scale
+    return [(ETA / WHOLE) * lax.rsqrt(norm(k) + EPSILON) for k in range(2)]
+
+
+def finish(
+    cells,
+    density,
+    pull,
+    lower,
+    upper,
+    slowness,
+    push,
+    lines,
+    density_out,
+    slowness_out,
+    objective,
+    density_new,
+    slowness_new,
+    sem,
+):
+    step_density, step_slowness = steps_of(lines[ITERS - 1], cells)
+    pieces = 4
+    length = density.shape[0] // pieces
+    copies = []
+    for k in range(pieces):
+        span = pl.ds(k * length, length)
+
+        def body(x, carry):
+            moved = density[x] - step_density * pull[x]
+            density_new[x] = jnp.minimum(jnp.maximum(moved, lower[x]), upper[x])
+            slowness_new[x] = slowness[x] - step_slowness * push[x]
+            return carry
+
+        lax.fori_loop(k * length, (k + 1) * length, body, 0, unroll=2)
+        for source, target in ((density_new, density_out), (slowness_new, slowness_out)):
+            copies.append(
+                pltpu.make_async_copy(source.at[span], target.at[span], sem.at[len(copies)])
+            )
+            copies[-1].start()
+    lane = lax.broadcasted_iota(jnp.int32, (1, lines.shape[-1]), 1)
+    pick = lambda phase, k: jnp.where(lane == k, lines[phase], 0.0)
+    for phase in range(ITERS):
+        parts = pick(phase, 2)
+        if phase < ITERS - 1:
+            parts = parts + pick(phase + 1, 3)
+        objective[phase] = jnp.sum(parts) * (0.5 / cells)
+    for copy in copies:
+        copy.wait()
 
 
 def kernel(
@@ -43,8 +97,12 @@
     lows,
     highs,
     density_out,
+    pull_out,
+    lower_out,
+    upper_out,
     slowness_out,
-    objective,
+    push_out,
+    lines_out,
     field,
     grads,
     zone,
@@ -52,9 +110,9 @@
     upper,
     lever,
     twist,
+    twist_lhs,
     slope,
     turn,
-    cums,
     pulls,
     fixed,
     pobs,
@@ -62,6 +120,7 @@
     lhs,
     table,
     rev_table,
+    up_table,
     low_table,
     high_table,
     column_send,
@@ -137,9 +196,9 @@
     downward = jnp.where(row >= col, 1.0, 0.0).astype(jnp.bfloat16)
     for half in range(2):
         tall = pl.ds(half * depth, depth)
-        table[tall, pl.ds(0, depth)] = upward
-        table[tall, pl.ds(depth, depth)] = both
-        table[tall, pl.ds(2 * depth, depth)] = differ
+        table[tall, pl.ds(0, depth)] = both
+        table[tall, pl.ds(depth, depth)] = differ
+        up_table[tall, :] = upward
         rev_table[tall, :] = downward
 
     pl.semaphore_wait(barrier, len(greet))
@@ -251,12 +310,8 @@
         everyone = norm_recv.at[phase]
         pltpu.make_async_copy(everyone, everyone, norm_recv_sem.at[phase]).wait()
         line = jnp.sum(norm_recv[phase], axis=0) + norm_send[phase]
-        pick = lambda k: jnp.sum(jnp.where(lane == k, line, 0.0), axis=1, keepdims=True)
-        scale = 1.0 / (WHOLE * WHOLE * cells)
-        step_density = (ETA / WHOLE) * lax.rsqrt(pick(0) * scale + EPSILON)
-        step_slowness = (ETA / WHOLE) * lax.rsqrt(pick(1) * scale + EPSILON)
-        objective[phase] = jnp.sum(jnp.where(lane == 2, line, 0.0)) * (0.5 / cells)
-        return step_density, step_slowness
+        lines_out[phase] = line
+        return steps_of(line, cells)
 
     loads[0].wait()
     loads[1].wait()
@@ -279,9 +334,6 @@
     column_send[0, 0] = total
     column_send[0, 1] = xscale * (weighted + later_parts * total) - observed
     start_columns(0)
-    loads[3].wait()
-    zone_rims = rim_copies(zone, (), lambda k: zone_send.at[k], lambda k: zone_recv.at[k])
-    start_rims(zone_rims)
 
     loads[4].wait()
     planes = 8
@@ -297,28 +349,40 @@
 
     lax.fori_loop(0, sx // planes, fix, 0, unroll=2)
 
-    def integrate(step):
-        span = pl.ds(pl.multiple_of(step * planes, planes), planes)
-        flat = pl.ds(pl.multiple_of(step * tall, tall), tall)
-        out = jnp.dot(lhs[flat], table[...], preferred_element_type=jnp.float32)
-        for buffer, k in ((cums, 0), (pulls, 1), (slope.at[0], 2)):
-            buffer[span] = out[:, k * depth : (k + 1) * depth].reshape(planes, sy, depth)
-
-    def in_steps(prepare):
-        prepare(0)
-
-        def body(step, carry):
-            integrate(step - 1)
-            prepare(step)
-            return carry
-
-        lax.fori_loop(1, sx // planes, body, 0)
-        integrate(sx // planes - 1)
+    long = min(LONG, sx)
+
+    def integrate():
+        for step in range(sx // long):
+            span = pl.ds(step * long, long)
+            out = jnp.dot(
+                lhs[pl.ds(step * long * sy, long * sy)],
+                table[...],
+                preferred_element_type=jnp.float32,
+            )
+            pulls[span] = out[:, :depth].reshape(long, sy, depth)
+            slope[0, span] = out[:, depth:].reshape(long, sy, depth)
+
+    def fits():
+        def body(step, squares):
+            out = jnp.dot(
+                lhs[pl.ds(pl.multiple_of(step * long * sy, 8), long * sy)],
+                up_table[...],
+                preferred_element_type=jnp.float32,
+            )
+            miss = out - pobs[pl.ds(step * long, long)].reshape(long * sy, depth)
+            return squares + jnp.sum((miss * miss).reshape(long * sy // 8, 8, depth), axis=0)
+
+        return lax.fori_loop(0, sx // long, body, zero_tile)
 
     def fill(step, values):
         lhs[pl.ds(pl.multiple_of(step * tall, tall), tall)] = halves(values.reshape(tall, depth))
 
-    in_steps(lambda k: fill(k, field[0, pl.ds(pl.multiple_of(k * planes, planes) + RIM, planes), own_y]))
+    def first_fill(k, carry):
+        fill(k, field[0, pl.ds(pl.multiple_of(k * planes, planes) + RIM, planes), own_y])
+        return carry
+
+    lax.fori_loop(0, sx // planes, first_fill, 0)
+    integrate()
 
     def all_slopes(source, target):
         def body(step, carry):
@@ -380,6 +444,7 @@
         p = x + RIM
         center = [[field[f, p, rows(j)] for j in range(-1, groups + 1)] for f in range(2)]
         squares = []
+        twists = [], []
         for j in range(groups):
             first_vec, second_vec = [
                 (
@@ -393,8 +458,13 @@
             for f, vec in ((0, cross(second_vec, crossed)), (1, cross(crossed, first_vec))):
                 lever[2 * f, p, rows(j)] = vec[0]
                 lever[2 * f + 1, p, rows(j)] = vec[1]
-                twist[f, x + BATCH, own(j)] = vec[2]
+                twists[f].append(vec[2])
             squares.append(tree([c * c for c in crossed]))
+        for f in range(2):
+            for j in range(0, groups, 2):
+                twist_lhs[f, pl.ds(pl.multiple_of(x * sy, 16) + 8 * j, 16)] = halves(
+                    jnp.concatenate(twists[f][j : j + 2], axis=0)
+                )
         first_vec, second_vec = [
             (
                 field[f, p + 1, ring] - field[f, p - 1, ring],
@@ -408,15 +478,18 @@
         lever[3, p, ring] = cross(crossed, first_vec)[1]
         return tree(squares)
 
-    def untwist(at):
+    def untwist():
         for f in range(2):
-            for k in range(BATCH):
-                for j in range(groups):
-                    twist[f, at + k, own(j)] = depth_difference(twist[f, at + k, own(j)])
+            for step in range(sx // long):
+                out = jnp.dot(
+                    twist_lhs[f, pl.ds(step * long * sy, long * sy)],
+                    table[:, pl.ds(depth, depth)],
+                    preferred_element_type=jnp.float32,
+                )
+                twist[f, pl.ds(step * long, long)] = out.reshape(long, sy, depth)
 
     def levers(step, squares):
         x = step * BATCH
-        untwist(x)
         return squares + tree([plane_levers(x + k) for k in range(BATCH)])
 
     def cross(u, v):
@@ -427,21 +500,26 @@
         along = [lever[2 * f + 1, p, rows(j)] for j in range(-1, groups + 1)]
         return [
             (lever[2 * f, p - 1, rows(j)] - lever[2 * f, p + 1, rows(j)])
-            + ((along[j] - along[j + 2]) - twist[f, x + BATCH, own(j)])
+            + ((along[j] - along[j + 2]) - twist[f, x, pl.ds(8 * j, 8)])
             for j in range(groups)
         ]
 
     before = ahead = None
+    fit_squares = late_squares = zero_tile
     rim_sets = [rims]
     for phase in range(ITERS):
         if phase == 0:
             arrived(rims)
         none = (zero_tile,) * groups
         crossed_squares = lax.fori_loop(0, sx // BATCH, levers, zero_tile)
-        untwist(sx)
         edge_levers(RIM - 1)
         edge_levers(RIM + sx)
-
+        untwist()
+
+        if phase == 0:
+            loads[3].wait()
+            zone_rims = rim_copies(zone, (), lambda k: zone_send.at[k], lambda k: zone_recv.at[k])
+            start_rims(zone_rims)
         columns_arrived(phase)
         earlier, later = columns_summed(phase)
         if phase == 0:
@@ -462,6 +540,8 @@
             sent(rim_sets[phase - 1])
         slot = phase % 2
 
+        if phase == ITERS - 1:
+            late_squares = fits()
         push_scale = WHOLE * xscale * xscale
 
         def descend(step, carry):
@@ -470,19 +550,24 @@
                 x = step * BATCH + k
                 p = x + RIM
                 spreads = spread(0, x), spread(1, x)
-                terms = [[], [], [], []]
+                terms = [[], [], []]
                 for j in range(groups):
-                    fit = cums[x, own(j)] - pobs[x, own(j)]
                     pull = (pulls[x, own(j)] - fixed[x, own(j)]) + spreads[0][j]
-                    grads[2 * slot, p, rows(j)] = pull
+                    if phase < ITERS - 1:
+                        grads[2 * slot, p, rows(j)] = pull
+                    else:
+                        pull_out[x, own(j)] = pull
                     running[j] = running[j] + field[1, p, rows(j)]
                     miss = running[j] - tobs[x, own(j)]
                     push = push_scale * push_sum[j] + spreads[1][j]
                     push_sum[j] = push_sum[j] - miss
-                    grads[2 * slot + 1, p, rows(j)] = push
+                    if phase < ITERS - 1:
+                        grads[2 * slot + 1, p, rows(j)] = push
+                    else:
+                        push_out[x, own(j)] = push
                     total[j] = total[j] + push
                     weighted[j] = weighted[j] + total[j]
-                    for term, value in zip(terms, (pull, push, fit, miss)):
+                    for term, value in zip(terms, (pull, push, miss)):
                         term.append(value * value)
                 squares = [square + tree(term) for square, term in zip(squares, terms)]
             return tuple(map(tuple, (running, push_sum, total, weighted, squares)))
@@ -490,7 +575,7 @@
         state[0] = before
         state[1] = ahead
         split = lambda k: tuple(state[k, own(j)] for j in range(groups))
-        carry = (split(0), split(1), none, none, (zero_tile,) * 4)
+        carry = (split(0), split(1), none, none, (zero_tile,) * 3)
         _, _, totals, weights, squares = lax.fori_loop(0, sx // BATCH, descend, carry)
         for j in range(groups):
             state[0, own(j)] = totals[j]
@@ -501,9 +586,10 @@
             (
                 squares[0],
                 squares[1],
-                squares[2] * (zscale * zscale)
-                + squares[3] * (xscale * xscale)
-                + crossed_squares * (1.0 / 16.0),
+                squares[2] * (xscale * xscale)
+                + crossed_squares * (1.0 / 16.0)
+                + late_squares * (zscale * zscale),
+                fit_squares * (zscale * zscale),
             ),
         )
         if phase < ITERS - 1:
@@ -527,6 +613,18 @@
             lax.fori_loop(0, px, look_up, 0)
         if phase < ITERS - 1:
             all_slopes(grads.at[2 * slot + 1], turn)
+            fit_squares = fits()
+        else:
+
+            def hand_over(x, carry):
+                p = x + RIM
+                density_out[x] = field[0, p, own_y]
+                slowness_out[x] = field[1, p, own_y]
+                lower_out[x] = lower[p, own_y]
+                upper_out[x] = upper[p, own_y]
+                return carry
+
+            lax.fori_loop(0, sx, hand_over, 0, unroll=2)
         step_density, step_slowness = norms(phase)
         if phase < ITERS - 1:
             arrived(new_rims)
@@ -539,7 +637,7 @@
             for p in (*range(RIM), *range(RIM + sx, px)):
                 move_rim(p, pl.ds(0, py))
 
-            def move(step):
+            def move(step, carry):
                 at = pl.multiple_of(step * planes, planes)
                 span = pl.ds(at + RIM, planes)
                 d = field[0, span, own_y] - step_density * grads[2 * slot, span, own_y]
@@ -555,19 +653,10 @@
                 for k in range(planes):
                     move_rim(at + RIM + k, pl.ds(0, PAD))
                     move_rim(at + RIM + k, pl.ds(PAD + sy, PAD))
-
-            in_steps(move)
-        else:
-
-            def finish(x, carry):
-                p = x + RIM
-                d = field[0, p, own_y] - step_density * grads[2 * slot, p, own_y]
-                density_out[x] = jnp.minimum(jnp.maximum(d, lower[p, own_y]), upper[p, own_y])
-                slowness_out[x] = field[1, p, own_y] - step_slowness * grads[2 * slot + 1, p, own_y]
                 return carry
 
-            lax.fori_loop(0, sx, finish, 0, unroll=2)
-
+            lax.fori_loop(0, sx // planes, move, 0)
+            integrate()
     sent(rim_sets[-1])
     for phase in range(ITERS):
         rest = column_recv.at[phase, pl.ds(0, nx - 1)]
@@ -589,11 +678,12 @@
         vmem = pl.BlockSpec(memory_space=pltpu.VMEM)
         dma = pltpu.SemaphoreType.DMA
         model = jax.ShapeDtypeStruct((sx, sy, depth), f32)
-        return pl.pallas_call(
+        inputs = (density, slowness, pressure, times, zones, low_table, high_table)
+        last = pl.pallas_call(
             functools.partial(kernel, nx, ny),
-            out_shape=(model, model, jax.ShapeDtypeStruct((ITERS,), f32)),
+            out_shape=(model,) * 6 + (jax.ShapeDtypeStruct((ITERS, 1, depth), f32),),
             in_specs=[hbm] * 7,
-            out_specs=(vmem, vmem, smem),
+            out_specs=(vmem,) * 7,
             scratch_shapes=[
                 pltpu.VMEM((2, px, py, depth), f32),
                 pltpu.VMEM((4, px, py, depth), f32),
@@ -601,11 +691,13 @@
                 pltpu.VMEM((px, py, depth), f32),
                 pltpu.VMEM((px, py, depth), f32),
                 pltpu.VMEM((4, px, py, depth), f32),
-                pltpu.VMEM((2, sx + BATCH, sy, depth), f32),
                 pltpu.VMEM((2, sx, sy, depth), f32),
-                *[pltpu.VMEM((sx, sy, depth), f32)] * 6,
+                pltpu.VMEM((2, sx * sy, 2 * depth), bf16),
+                pltpu.VMEM((2, sx, sy, depth), f32),
+                *[pltpu.VMEM((sx, sy, depth), f32)] * 5,
                 pltpu.VMEM((sx * sy, 2 * depth), bf16),
-                pltpu.VMEM((2 * depth, 3 * depth), bf16),
+                pltpu.VMEM((2 * depth, 2 * depth), bf16),
+                pltpu.VMEM((2 * depth, depth), bf16),
                 pltpu.VMEM((2 * depth, depth), bf16),
                 pltpu.SMEM(zones_shape, f32),
                 pltpu.SMEM(zones_shape, f32),
@@ -627,9 +719,21 @@
             compiler_params=pltpu.CompilerParams(
                 collective_id=0,
                 has_side_effects=True,
-                vmem_limit_bytes=54 * 1024 * 1024,
+                vmem_limit_bytes=44 * 1024 * 1024,
             ),
-        )(density, slowness, pressure, times, zones, low_table, high_table)
+        )(*[pltpu.with_memory_space_constraint(value, pltpu.HBM) for value in inputs])
+        return pl.pallas_call(
+            functools.partial(finish, float(nx * sx * ny * sy * depth)),
+            out_shape=(model, model, jax.ShapeDtypeStruct((ITERS,), f32)),
+            in_specs=[vmem] * 7,
+            out_specs=(pl.BlockSpec(memory_space=pl.ANY),) * 2 + (smem,),
+            scratch_shapes=[
+                pltpu.VMEM((sx, sy, depth), f32),
+                pltpu.VMEM((sx, sy, depth), f32),
+                dma((8,)),
+            ],
+            compiler_params=pltpu.CompilerParams(vmem_limit_bytes=8 * 1024 * 1024),
+        )(*last)
 
     part = P("gx", "gy", None)
     return jax.shard_map(

time: 59.2 us -> 52.1 us (0.88)
  local copies, waits for them, and re-layouts: 3.84 us -> 0 us
  Pallas kernels: 54.6 us -> 51.4 us
    unnamed x7 -> x0, local copies, waits for them, and re-layouts: 3.84 us -> none
    pallas_call x1 -> x2, Pallas kernels: 54.6 us -> 51.4 us  [the longest x1 49.3 us: local(): pl.pallas_call(functools.partial(kernel, nx, ny), out_shape=(model,) * 6...]
where the time goes in v3:
time: 52.1 us; the launch traced here: 52 us
  Pallas kernels  51.4 us (99%)
  between operations  0.64 us (1%)
    pallas_call x1, Pallas kernels, local(): pl.pallas_call(functools.partial(kernel, nx, ny), out_shape=(model,) * 6...  49.3 us
    pallas_call x1, Pallas kernels, local(): pl.pallas_call(functools.partial(finish, float(nx * sx * ny * sy * depth)...  2.09 us

profile of v3, /device:TPU:1, one launch (start us, length us, event | category | flops | bytes accessed | tf_op | source)
XLA Modules:
  0.0 52.0 jit_solution(4278399269583971485)
XLA Ops:
  0.6 49.3 %shard_map.94 = (f32[64,32,128]{2,1,0:T(8,128)S(1)}, f32[64,32,128]{2,1,0:T(8,128)S(1)}, f32[64,32,128]{2,1,0:T(8,128)S(1)}, f32[64,32,128]{2,1,0:T(8,128)S(1)},...) custom-call(f32[64,32,128]{2,1,0:T(8,128)} %density.1, f32[64,32,128]{2,1,0:T(8,128)} %slowness.1, ...), custom_call_target="tpu_custom_call" | custom-call | tf_op jit(solution)/shard_map/pallas_call | solution.py:682
  49.9 2.1 %shard_map.95 = (f32[64,32,128]{2,1,0:T(8,128)}, f32[64,32,128]{2,1,0:T(8,128)}, f32[3]{0:T(128)}) custom-call(f32[64,32,128]{2,1,0:T(8,128)S(1)} %get-tuple-element.10.density, f32[64,32,128]{2,1,0:T(8,128)S(1)} %get-tuple-element.11.pull, f32[64,32,128]{2,1,0:T(8,128)S(1)} %get-tuple-element.12.lower, f32[64,32,128]{2,1,0:T(8,128)S(1)} %get-tuple-element.13.upper, ...), custom_call_target="tpu_custom_call" | custom-call | tf_op jit(solution)/shard_map/pallas_call | solution.py:725

commit v4 on v3

--- a/solution.py
+++ b/solution.py
@@ -16,7 +16,7 @@
 RIM = 2
 LONG = 32
 WHOLE = 16.0
-BATCH = 4
+BATCH = 8
 
 
 def depth_difference(values):
@@ -57,7 +57,7 @@
     sem,
 ):
     step_density, step_slowness = steps_of(lines[ITERS - 1], cells)
-    pieces = 4
+    pieces = 8
     length = density.shape[0] // pieces
     copies = []
     for k in range(pieces):
@@ -161,11 +161,19 @@
     def turned(value, step, size):
         return lax.rem(value + step, size)
 
+    near = [0, 1, 2, 1]
+
+    def far_first(steps):
+        if (nx, ny) == (16, 8):
+            steps = sorted(steps, key=lambda t: -(near[t[0] // 4] + near[t[0] % 4] + near[t[1] // 2]))
+        return steps
+
     barrier = pltpu.get_barrier_semaphore()
-    greet = [(turned(gx, k, nx), gy) for k in range(1, nx)]
-    greet += [(gx, turned(gy, k, ny)) for k in range(1, ny)]
-    greet += [(turned(gx, i, nx), turned(gy, j, ny)) for i in (1, nx - 1) for j in (1, ny - 1)]
-    for device in greet:
+    steps_x = [i for i, _ in far_first([(i, 0) for i in range(1, nx)])]
+    greet = [(i, 0) for i in range(1, nx)] + [(0, j) for j in range(1, ny)]
+    greet += [(i, j) for i in (1, nx - 1) for j in (1, ny - 1)]
+    for i, j in far_first(greet):
+        device = (turned(gx, i, nx), turned(gy, j, ny))
         pl.semaphore_signal(barrier, inc=1, device_id=device, device_id_type=MESH)
 
     @pl.when(gy == 0)
@@ -198,9 +206,25 @@
         tall = pl.ds(half * depth, depth)
         table[tall, pl.ds(0, depth)] = both
         table[tall, pl.ds(depth, depth)] = differ
+        table[tall, pl.ds(2 * depth, depth)] = upward
         up_table[tall, :] = upward
         rev_table[tall, :] = downward
 
+    loads[0].wait()
+    loads[1].wait()
+
+    def first_sums(x, carry):
+        running, weighted, observed = carry
+        running = running + field[1, x + RIM, own_y]
+        seen = tobs[x]
+        tobs[x] = seen * (1.0 / xscale)
+        return running, weighted + running, observed + seen
+
+    zero = jnp.zeros((sy, depth), jnp.float32)
+    total, weighted, observed = lax.fori_loop(0, sx, first_sums, (zero, zero, zero), unroll=4)
+    later_parts = (nx - 1 - gx).astype(jnp.float32) * float(sx)
+    column_send[0, 0] = total
+    column_send[0, 1] = xscale * (weighted + later_parts * total) - observed
     pl.semaphore_wait(barrier, len(greet))
 
     def rim_copies(buffer, lead, send_sems, recv_sems):
@@ -245,7 +269,7 @@
         return copies
 
     def start_rims(copies):
-        for sends, _, copy in copies:
+        for sends, _, copy in copies[4:] + copies[:4]:
             pl.when(sends)(copy.start)
 
     def arrived(copies):
@@ -257,7 +281,7 @@
             pl.when(sends)(copy.wait_send)
 
     def start_columns(phase):
-        for k in range(1, nx):
+        for k in steps_x:
             to = turned(gx, k, nx)
             pltpu.make_async_remote_copy(
                 src_ref=column_send.at[phase, jnp.where(to > gx, 0, 1)],
@@ -281,11 +305,8 @@
             later = later + jnp.where(gx < k, value, 0.0)
         return earlier, later
 
-    near = [0, 1, 2, 1]
     lane = lax.broadcasted_iota(jnp.int32, (1, depth), 1)
-    steps = [(i, j) for i in range(nx) for j in range(ny) if i or j]
-    if nx == 16 and ny == 8:
-        steps.sort(key=lambda t: -(near[t[0] // 4] + near[t[0] % 4] + near[t[1] // 2]))
+    steps = far_first([(i, j) for i in range(nx) for j in range(ny) if i or j])
     others = nx * ny - 1
 
     def start_norms(phase, values):
@@ -299,7 +320,7 @@
         for i, j in steps:
             pltpu.make_async_remote_copy(
                 src_ref=norm_send.at[phase],
-                dst_ref=norm_recv.at[phase, i * ny + j - 1],
+                dst_ref=norm_recv.at[phase, pl.ds(i * ny + j, 1)],
                 send_sem=norm_send_sem.at[phase],
                 recv_sem=norm_recv_sem.at[phase],
                 device_id=(to_x[i], to_y[j]),
@@ -307,32 +328,18 @@
             ).start()
 
     def norms(phase):
-        everyone = norm_recv.at[phase]
-        pltpu.make_async_copy(everyone, everyone, norm_recv_sem.at[phase]).wait()
-        line = jnp.sum(norm_recv[phase], axis=0) + norm_send[phase]
+        rest = norm_recv.at[phase, pl.ds(1, others)]
+        pltpu.make_async_copy(rest, rest, norm_recv_sem.at[phase]).wait()
+        norm_recv[phase, 0:1] = norm_send[phase]
+        line = jnp.sum(norm_recv[phase], axis=0, keepdims=True)
         lines_out[phase] = line
         return steps_of(line, cells)
 
-    loads[0].wait()
-    loads[1].wait()
-
-    def first_sums(x, carry):
-        running, weighted, observed = carry
-        running = running + field[1, x + RIM, own_y]
-        seen = tobs[x]
-        tobs[x] = seen * (1.0 / xscale)
-        return running, weighted + running, observed + seen
-
-    zero = jnp.zeros((sy, depth), jnp.float32)
     loads[2].wait()
     rims = rim_copies(
         field, (pl.ds(0, 2),), lambda k: rim_send.at[0, k], lambda k: rim_recv.at[0, k]
     )
     start_rims(rims)
-    total, weighted, observed = lax.fori_loop(0, sx, first_sums, (zero, zero, zero), unroll=4)
-    later_parts = (nx - 1 - gx).astype(jnp.float32) * float(sx)
-    column_send[0, 0] = total
-    column_send[0, 1] = xscale * (weighted + later_parts * total) - observed
     start_columns(0)
 
     loads[4].wait()
@@ -351,16 +358,19 @@
 
     long = min(LONG, sx)
 
-    def integrate():
+    def integrate(last):
+        width = (3 if last else 2) * depth
         for step in range(sx // long):
             span = pl.ds(step * long, long)
             out = jnp.dot(
                 lhs[pl.ds(step * long * sy, long * sy)],
-                table[...],
+                table[:, pl.ds(0, width)],
                 preferred_element_type=jnp.float32,
             )
             pulls[span] = out[:, :depth].reshape(long, sy, depth)
-            slope[0, span] = out[:, depth:].reshape(long, sy, depth)
+            slope[0, span] = out[:, depth : 2 * depth].reshape(long, sy, depth)
+            if last:
+                turn[span] = out[:, 2 * depth :].reshape(long, sy, depth)
 
     def fits():
         def body(step, squares):
@@ -382,7 +392,7 @@
         return carry
 
     lax.fori_loop(0, sx // planes, first_fill, 0)
-    integrate()
+    integrate(False)
 
     def all_slopes(source, target):
         def body(step, carry):
@@ -394,16 +404,24 @@
 
     all_slopes(field.at[1], slope.at[1])
 
-    def look_up(x, carry):
-        number = zone[x]
+    def look_up(p, at):
+        number = zone[p, at]
         low = jnp.zeros(number.shape, jnp.float32)
         high = low
-        for k in range(low_table.shape[0]):
+        for k in range(lows.shape[0]):
             hit = number == k
             low = jnp.where(hit, low_table[k], low)
             high = jnp.where(hit, high_table[k], high)
-        lower[x] = low
-        upper[x] = high
+        lower[p, at] = low
+        upper[p, at] = high
+
+    def own_look_up(x, carry):
+        look_up(x + RIM, own_y)
+        return carry
+
+    def rim_look_up(x, carry):
+        look_up(x + RIM, pl.ds(0, PAD))
+        look_up(x + RIM, pl.ds(PAD + sy, PAD))
         return carry
 
     groups = sy // 8
@@ -462,7 +480,7 @@
             squares.append(tree([c * c for c in crossed]))
         for f in range(2):
             for j in range(0, groups, 2):
-                twist_lhs[f, pl.ds(pl.multiple_of(x * sy, 16) + 8 * j, 16)] = halves(
+                twist_lhs[f, pl.ds(pl.multiple_of((x + BATCH) * sy, 16) + 8 * j, 16)] = halves(
                     jnp.concatenate(twists[f][j : j + 2], axis=0)
                 )
         first_vec, second_vec = [
@@ -478,18 +496,18 @@
         lever[3, p, ring] = cross(crossed, first_vec)[1]
         return tree(squares)
 
-    def untwist():
+    def untwist(x):
         for f in range(2):
-            for step in range(sx // long):
-                out = jnp.dot(
-                    twist_lhs[f, pl.ds(step * long * sy, long * sy)],
-                    table[:, pl.ds(depth, depth)],
-                    preferred_element_type=jnp.float32,
-                )
-                twist[f, pl.ds(step * long, long)] = out.reshape(long, sy, depth)
+            out = jnp.dot(
+                twist_lhs[f, pl.ds(pl.multiple_of(x * sy, 16), BATCH * sy)],
+                table[:, pl.ds(depth, depth)],
+                preferred_element_type=jnp.float32,
+            )
+            twist[f, pl.ds(x, BATCH)] = out.reshape(BATCH, sy, depth)
 
     def levers(step, squares):
         x = step * BATCH
+        untwist(x)
         return squares + tree([plane_levers(x + k) for k in range(BATCH)])
 
     def cross(u, v):
@@ -500,26 +518,27 @@
         along = [lever[2 * f + 1, p, rows(j)] for j in range(-1, groups + 1)]
         return [
             (lever[2 * f, p - 1, rows(j)] - lever[2 * f, p + 1, rows(j)])
-            + ((along[j] - along[j + 2]) - twist[f, x, pl.ds(8 * j, 8)])
+            + ((along[j] - along[j + 2]) - twist[f, x + BATCH, pl.ds(8 * j, 8)])
             for j in range(groups)
         ]
 
+    fit_squares = fits()
+    for k in (3, 5, 6):
+        loads[k].wait()
+    lax.fori_loop(0, sx, own_look_up, 0)
     before = ahead = None
-    fit_squares = late_squares = zero_tile
     rim_sets = [rims]
     for phase in range(ITERS):
         if phase == 0:
             arrived(rims)
+            zone_rims = rim_copies(zone, (), lambda k: zone_send.at[k], lambda k: zone_recv.at[k])
+            start_rims(zone_rims)
         none = (zero_tile,) * groups
         crossed_squares = lax.fori_loop(0, sx // BATCH, levers, zero_tile)
         edge_levers(RIM - 1)
         edge_levers(RIM + sx)
-        untwist()
-
-        if phase == 0:
-            loads[3].wait()
-            zone_rims = rim_copies(zone, (), lambda k: zone_send.at[k], lambda k: zone_recv.at[k])
-            start_rims(zone_rims)
+        untwist(sx)
+
         columns_arrived(phase)
         earlier, later = columns_summed(phase)
         if phase == 0:
@@ -540,8 +559,6 @@
             sent(rim_sets[phase - 1])
         slot = phase % 2
 
-        if phase == ITERS - 1:
-            late_squares = fits()
         push_scale = WHOLE * xscale * xscale
 
         def descend(step, carry):
@@ -550,7 +567,7 @@
                 x = step * BATCH + k
                 p = x + RIM
                 spreads = spread(0, x), spread(1, x)
-                terms = [[], [], []]
+                terms = [[] for _ in squares]
                 for j in range(groups):
                     pull = (pulls[x, own(j)] - fixed[x, own(j)]) + spreads[0][j]
                     if phase < ITERS - 1:
@@ -567,7 +584,10 @@
                         push_out[x, own(j)] = push
                     total[j] = total[j] + push
                     weighted[j] = weighted[j] + total[j]
-                    for term, value in zip(terms, (pull, push, miss)):
+                    values = (pull, push, miss)
+                    if phase == ITERS - 1:
+                        values += (turn[x, own(j)] - pobs[x, own(j)],)
+                    for term, value in zip(terms, values):
                         term.append(value * value)
                 squares = [square + tree(term) for square, term in zip(squares, terms)]
             return tuple(map(tuple, (running, push_sum, total, weighted, squares)))
@@ -575,7 +595,7 @@
         state[0] = before
         state[1] = ahead
         split = lambda k: tuple(state[k, own(j)] for j in range(groups))
-        carry = (split(0), split(1), none, none, (zero_tile,) * 3)
+        carry = (split(0), split(1), none, none, (zero_tile,) * (3 if phase < ITERS - 1 else 4))
         _, _, totals, weights, squares = lax.fori_loop(0, sx // BATCH, descend, carry)
         for j in range(groups):
             state[0, own(j)] = totals[j]
@@ -588,7 +608,7 @@
                 squares[1],
                 squares[2] * (xscale * xscale)
                 + crossed_squares * (1.0 / 16.0)
-                + late_squares * (zscale * zscale),
+                + (squares[3] * (zscale * zscale) if phase == ITERS - 1 else 0.0),
                 fit_squares * (zscale * zscale),
             ),
         )
@@ -603,17 +623,11 @@
             start_rims(new_rims)
             column_send[phase + 1, 0] = total
             column_send[phase + 1, 1] = weighted + later_parts * total
-            start_columns(phase + 1)
-        if phase == 0:
-            sent(rims)
-            arrived(zone_rims)
-            sent(zone_rims)
-            loads[5].wait()
-            loads[6].wait()
-            lax.fori_loop(0, px, look_up, 0)
         if phase < ITERS - 1:
             all_slopes(grads.at[2 * slot + 1], turn)
-            fit_squares = fits()
+            start_columns(phase + 1)
+            if phase > 0:
+                fit_squares = fits()
         else:
 
             def hand_over(x, carry):
@@ -625,6 +639,13 @@
                 return carry
 
             lax.fori_loop(0, sx, hand_over, 0, unroll=2)
+        if phase == 0:
+            sent(rims)
+            arrived(zone_rims)
+            sent(zone_rims)
+            lax.fori_loop(0, sx, rim_look_up, 0, unroll=2)
+            for p in (*range(RIM), *range(RIM + sx, px)):
+                look_up(p, pl.ds(0, py))
         step_density, step_slowness = norms(phase)
         if phase < ITERS - 1:
             arrived(new_rims)
@@ -656,13 +677,13 @@
                 return carry
 
             lax.fori_loop(0, sx // planes, move, 0)
-            integrate()
+            integrate(phase == ITERS - 2)
     sent(rim_sets[-1])
     for phase in range(ITERS):
         rest = column_recv.at[phase, pl.ds(0, nx - 1)]
         pltpu.make_async_copy(rest, rest, col_send_sem.at[phase]).wait()
-        everyone = norm_recv.at[phase]
-        pltpu.make_async_copy(everyone, everyone, norm_send_sem.at[phase]).wait()
+        rest = norm_recv.at[phase, pl.ds(1, others)]
+        pltpu.make_async_copy(rest, rest, norm_send_sem.at[phase]).wait()
 
 
 def solution(mesh):
@@ -691,12 +712,12 @@
                 pltpu.VMEM((px, py, depth), f32),
                 pltpu.VMEM((px, py, depth), f32),
                 pltpu.VMEM((4, px, py, depth), f32),
-                pltpu.VMEM((2, sx, sy, depth), f32),
-                pltpu.VMEM((2, sx * sy, 2 * depth), bf16),
+                pltpu.VMEM((2, sx + BATCH, sy, depth), f32),
+                pltpu.VMEM((2, (sx + BATCH) * sy, 2 * depth), bf16),
                 pltpu.VMEM((2, sx, sy, depth), f32),
                 *[pltpu.VMEM((sx, sy, depth), f32)] * 5,
                 pltpu.VMEM((sx * sy, 2 * depth), bf16),
-                pltpu.VMEM((2 * depth, 2 * depth), bf16),
+                pltpu.VMEM((2 * depth, 3 * depth), bf16),
                 pltpu.VMEM((2 * depth, depth), bf16),
                 pltpu.VMEM((2 * depth, depth), bf16),
                 pltpu.SMEM(zones_shape, f32),
@@ -704,7 +725,7 @@
                 pltpu.VMEM((ITERS, 2, sy, depth), f32),
                 pltpu.VMEM((ITERS, nx, sy, depth), f32),
                 pltpu.VMEM((ITERS, 1, depth), f32),
-                pltpu.VMEM((ITERS, nx * ny - 1, 1, depth), f32),
+                pltpu.VMEM((ITERS, nx * ny, depth), f32),
                 dma((7,)),
                 dma((ITERS, 8)),
                 dma((ITERS, 8)),
@@ -730,7 +751,7 @@
             scratch_shapes=[
                 pltpu.VMEM((sx, sy, depth), f32),
                 pltpu.VMEM((sx, sy, depth), f32),
-                dma((8,)),
+                dma((16,)),
             ],
             compiler_params=pltpu.CompilerParams(vmem_limit_bytes=8 * 1024 * 1024),
         )(*last)

time: 52.1 us -> 50.1 us (0.962)
  Pallas kernels: 51.4 us -> 49.4 us
    pallas_call x1, Pallas kernels: 49.3 us -> 47.3 us  [local(): pl.pallas_call(functools.partial(kernel, nx, ny), out_shape=(model,) * 6...]
where the time goes in v4:
time: 50.1 us; the launch traced here: 50 us
  Pallas kernels  49.4 us (99%)
  between operations  0.64 us (1%)
    pallas_call x1, Pallas kernels, local(): pl.pallas_call(functools.partial(kernel, nx, ny), out_shape=(model,) * 6...  47.3 us
    pallas_call x1, Pallas kernels, local(): pl.pallas_call(functools.partial(finish, float(nx * sx * ny * sy * depth)...  2.1 us

profile of v4, /device:TPU:1, one launch (start us, length us, event | category | flops | bytes accessed | tf_op | source)
XLA Modules:
  0.0 50.0 jit_solution(15538372712268657010)
XLA Ops:
  0.6 47.3 %shard_map.94 = (f32[64,32,128]{2,1,0:T(8,128)S(1)}, f32[64,32,128]{2,1,0:T(8,128)S(1)}, f32[64,32,128]{2,1,0:T(8,128)S(1)}, f32[64,32,128]{2,1,0:T(8,128)S(1)},...) custom-call(f32[64,32,128]{2,1,0:T(8,128)} %density.1, f32[64,32,128]{2,1,0:T(8,128)} %slowness.1, ...), custom_call_target="tpu_custom_call" | custom-call | tf_op jit(solution)/shard_map/pallas_call | solution.py:703
  47.9 2.1 %shard_map.95 = (f32[64,32,128]{2,1,0:T(8,128)}, f32[64,32,128]{2,1,0:T(8,128)}, f32[3]{0:T(128)}) custom-call(f32[64,32,128]{2,1,0:T(8,128)S(1)} %get-tuple-element.10.density, f32[64,32,128]{2,1,0:T(8,128)S(1)} %get-tuple-element.11.pull, f32[64,32,128]{2,1,0:T(8,128)S(1)} %get-tuple-element.12.lower, f32[64,32,128]{2,1,0:T(8,128)S(1)} %get-tuple-element.13.upper, ...), custom_call_target="tpu_custom_call" | custom-call | tf_op jit(solution)/shard_map/pallas_call | solution.py:746

commit v5 on v4

--- a/solution.py
+++ b/solution.py
@@ -54,12 +54,13 @@
     objective,
     density_new,
     slowness_new,
+    history,
     sem,
 ):
     step_density, step_slowness = steps_of(lines[ITERS - 1], cells)
     pieces = 8
     length = density.shape[0] // pieces
-    copies = []
+    pairs = ((density_new, density_out, sem.at[0]), (slowness_new, slowness_out, sem.at[1]))
     for k in range(pieces):
         span = pl.ds(k * length, length)
 
@@ -70,20 +71,20 @@
             return carry
 
         lax.fori_loop(k * length, (k + 1) * length, body, 0, unroll=2)
-        for source, target in ((density_new, density_out), (slowness_new, slowness_out)):
-            copies.append(
-                pltpu.make_async_copy(source.at[span], target.at[span], sem.at[len(copies)])
-            )
-            copies[-1].start()
+        for source, target, done in pairs:
+            pltpu.make_async_copy(source.at[span], target.at[span], done).start()
     lane = lax.broadcasted_iota(jnp.int32, (1, lines.shape[-1]), 1)
     pick = lambda phase, k: jnp.where(lane == k, lines[phase], 0.0)
     for phase in range(ITERS):
         parts = pick(phase, 2)
         if phase < ITERS - 1:
             parts = parts + pick(phase + 1, 3)
-        objective[phase] = jnp.sum(parts) * (0.5 / cells)
-    for copy in copies:
-        copy.wait()
+        history[phase] = jnp.sum(parts) * (0.5 / cells)
+    copy = pltpu.make_async_copy(history, objective, sem.at[2])
+    copy.start()
+    for source, target, done in pairs:
+        pltpu.make_async_copy(source, target, done).wait()
+    copy.wait()
 
 
 def kernel(
@@ -111,6 +112,7 @@
     lever,
     twist,
     twist_lhs,
+    kept,
     slope,
     turn,
     pulls,
@@ -130,7 +132,6 @@
     load_sem,
     rim_send,
     rim_recv,
-    zone_send,
     zone_recv,
     col_send_sem,
     col_recv_sem,
@@ -286,15 +287,16 @@
             pltpu.make_async_remote_copy(
                 src_ref=column_send.at[phase, jnp.where(to > gx, 0, 1)],
                 dst_ref=column_recv.at[phase, gx],
-                send_sem=col_send_sem.at[phase],
-                recv_sem=col_recv_sem.at[phase],
+                send_sem=col_send_sem,
+                recv_sem=col_recv_sem.at[phase % 2],
                 device_id=(to, gy),
                 device_id_type=MESH,
             ).start()
 
     def columns_arrived(phase):
         rest = column_recv.at[phase, pl.ds(0, nx - 1)]
-        pltpu.make_async_copy(rest, rest, col_recv_sem.at[phase]).wait()
+        pltpu.make_async_copy(rest, rest, col_recv_sem.at[phase % 2]).wait()
+        pltpu.make_async_copy(rest, rest, col_send_sem).wait()
 
     def columns_summed(phase):
         zero = jnp.zeros((sy, depth), jnp.float32)
@@ -321,15 +323,16 @@
             pltpu.make_async_remote_copy(
                 src_ref=norm_send.at[phase],
                 dst_ref=norm_recv.at[phase, pl.ds(i * ny + j, 1)],
-                send_sem=norm_send_sem.at[phase],
-                recv_sem=norm_recv_sem.at[phase],
+                send_sem=norm_send_sem,
+                recv_sem=norm_recv_sem.at[phase % 2],
                 device_id=(to_x[i], to_y[j]),
                 device_id_type=MESH,
             ).start()
 
     def norms(phase):
         rest = norm_recv.at[phase, pl.ds(1, others)]
-        pltpu.make_async_copy(rest, rest, norm_recv_sem.at[phase]).wait()
+        pltpu.make_async_copy(rest, rest, norm_recv_sem.at[phase % 2]).wait()
+        pltpu.make_async_copy(rest, rest, norm_send_sem).wait()
         norm_recv[phase, 0:1] = norm_send[phase]
         line = jnp.sum(norm_recv[phase], axis=0, keepdims=True)
         lines_out[phase] = line
@@ -337,7 +340,7 @@
 
     loads[2].wait()
     rims = rim_copies(
-        field, (pl.ds(0, 2),), lambda k: rim_send.at[0, k], lambda k: rim_recv.at[0, k]
+        field, (pl.ds(0, 2),), lambda k: rim_send.at[k], lambda k: rim_recv.at[0, k]
     )
     start_rims(rims)
     start_columns(0)
@@ -458,7 +461,7 @@
             lever[0, p, rows(j)] = cross(second_vec, crossed)[0]
             lever[2, p, rows(j)] = cross(crossed, first_vec)[0]
 
-    def plane_levers(x):
+    def plane_levers(x, last):
         p = x + RIM
         center = [[field[f, p, rows(j)] for j in range(-1, groups + 1)] for f in range(2)]
         squares = []
@@ -477,7 +480,11 @@
                 lever[2 * f, p, rows(j)] = vec[0]
                 lever[2 * f + 1, p, rows(j)] = vec[1]
                 twists[f].append(vec[2])
-            squares.append(tree([c * c for c in crossed]))
+            if last:
+                squares.append(tree([c * c for c in crossed]))
+            else:
+                for k, value in enumerate(crossed):
+                    kept[k, x, pl.ds(8 * j, 8)] = value
         for f in range(2):
             for j in range(0, groups, 2):
                 twist_lhs[f, pl.ds(pl.multiple_of((x + BATCH) * sy, 16) + 8 * j, 16)] = halves(
@@ -494,7 +501,7 @@
         crossed = cross(first_vec, second_vec)
         lever[1, p, ring] = cross(second_vec, crossed)[1]
         lever[3, p, ring] = cross(crossed, first_vec)[1]
-        return tree(squares)
+        return tree(squares) if last else None
 
     def untwist(x):
         for f in range(2):
@@ -505,13 +512,25 @@
             )
             twist[f, pl.ds(x, BATCH)] = out.reshape(BATCH, sy, depth)
 
-    def levers(step, squares):
+    def levers(last, step, squares):
         x = step * BATCH
         untwist(x)
-        return squares + tree([plane_levers(x + k) for k in range(BATCH)])
+        parts = [plane_levers(x + k, last) for k in range(BATCH)]
+        return squares + tree(parts) if last else squares
 
     def cross(u, v):
         return (u[1] * v[2] - u[2] * v[1], u[2] * v[0] - u[0] * v[2], u[0] * v[1] - u[1] * v[0])
+
+    def kept_squares():
+        def body(step, squares):
+            x = step * 4
+            sums = [
+                tree([jnp.sum((kept[k, x + i] ** 2).reshape(sy // 8, 8, depth), axis=0) for i in range(4)])
+                for k in range(3)
+            ]
+            return squares + tree(sums)
+
+        return lax.fori_loop(0, sx // 4, body, zero_tile)
 
     def spread(f, x):
         p = x + RIM
@@ -522,19 +541,20 @@
             for j in range(groups)
         ]
 
-    fit_squares = fits()
-    for k in (3, 5, 6):
-        loads[k].wait()
-    lax.fori_loop(0, sx, own_look_up, 0)
+    late_parts = zero_tile
+    loads[3].wait()
     before = ahead = None
     rim_sets = [rims]
     for phase in range(ITERS):
         if phase == 0:
             arrived(rims)
-            zone_rims = rim_copies(zone, (), lambda k: zone_send.at[k], lambda k: zone_recv.at[k])
+            sent(rims)
+            zone_rims = rim_copies(zone, (), lambda k: rim_send.at[k], lambda k: zone_recv.at[k])
             start_rims(zone_rims)
         none = (zero_tile,) * groups
-        crossed_squares = lax.fori_loop(0, sx // BATCH, levers, zero_tile)
+        crossed_squares = lax.fori_loop(
+            0, sx // BATCH, functools.partial(levers, phase == ITERS - 1), zero_tile
+        )
         edge_levers(RIM - 1)
         edge_levers(RIM + sx)
         untwist(sx)
@@ -555,8 +575,10 @@
             )
             before = before - step_slowness * earlier
 
-        if phase > 1:
-            sent(rim_sets[phase - 1])
+        if phase == 0:
+            sent(zone_rims)
+        else:
+            sent(rim_sets[phase])
         slot = phase % 2
 
         push_scale = WHOLE * xscale * xscale
@@ -609,15 +631,15 @@
                 squares[2] * (xscale * xscale)
                 + crossed_squares * (1.0 / 16.0)
                 + (squares[3] * (zscale * zscale) if phase == ITERS - 1 else 0.0),
-                fit_squares * (zscale * zscale),
+                late_parts,
             ),
         )
         if phase < ITERS - 1:
             new_rims = rim_copies(
                 grads,
                 (pl.ds(2 * slot, 2),),
-                lambda k, phase=phase: rim_send.at[phase + 1, k],
-                lambda k, phase=phase: rim_recv.at[phase + 1, k],
+                lambda k: rim_send.at[k],
+                lambda k, phase=phase: rim_recv.at[(phase + 1) % 2, k],
             )
             rim_sets.append(new_rims)
             start_rims(new_rims)
@@ -626,8 +648,7 @@
         if phase < ITERS - 1:
             all_slopes(grads.at[2 * slot + 1], turn)
             start_columns(phase + 1)
-            if phase > 0:
-                fit_squares = fits()
+            late_parts = fits() * (zscale * zscale) + kept_squares() * (1.0 / 16.0)
         else:
 
             def hand_over(x, carry):
@@ -640,9 +661,10 @@
 
             lax.fori_loop(0, sx, hand_over, 0, unroll=2)
         if phase == 0:
-            sent(rims)
+            loads[5].wait()
+            loads[6].wait()
+            lax.fori_loop(0, sx, own_look_up, 0)
             arrived(zone_rims)
-            sent(zone_rims)
             lax.fori_loop(0, sx, rim_look_up, 0, unroll=2)
             for p in (*range(RIM), *range(RIM + sx, px)):
                 look_up(p, pl.ds(0, py))
@@ -678,12 +700,6 @@
 
             lax.fori_loop(0, sx // planes, move, 0)
             integrate(phase == ITERS - 2)
-    sent(rim_sets[-1])
-    for phase in range(ITERS):
-        rest = column_recv.at[phase, pl.ds(0, nx - 1)]
-        pltpu.make_async_copy(rest, rest, col_send_sem.at[phase]).wait()
-        rest = norm_recv.at[phase, pl.ds(1, others)]
-        pltpu.make_async_copy(rest, rest, norm_send_sem.at[phase]).wait()
 
 
 def solution(mesh):
@@ -695,7 +711,6 @@
         px, py = sx + 2 * RIM, sy + 2 * PAD
         f32, bf16 = jnp.float32, jnp.bfloat16
         hbm = pl.BlockSpec(memory_space=pltpu.HBM)
-        smem = pl.BlockSpec(memory_space=pltpu.SMEM)
         vmem = pl.BlockSpec(memory_space=pltpu.VMEM)
         dma = pltpu.SemaphoreType.DMA
         model = jax.ShapeDtypeStruct((sx, sy, depth), f32)
@@ -714,6 +729,7 @@
                 pltpu.VMEM((4, px, py, depth), f32),
                 pltpu.VMEM((2, sx + BATCH, sy, depth), f32),
                 pltpu.VMEM((2, (sx + BATCH) * sy, 2 * depth), bf16),
+                pltpu.VMEM((3, sx, sy, depth), f32),
                 pltpu.VMEM((2, sx, sy, depth), f32),
                 *[pltpu.VMEM((sx, sy, depth), f32)] * 5,
                 pltpu.VMEM((sx * sy, 2 * depth), bf16),
@@ -727,31 +743,31 @@
                 pltpu.VMEM((ITERS, 1, depth), f32),
                 pltpu.VMEM((ITERS, nx * ny, depth), f32),
                 dma((7,)),
-                dma((ITERS, 8)),
-                dma((ITERS, 8)),
                 dma((8,)),
+                dma((2, 8)),
                 dma((8,)),
-                dma((ITERS,)),
-                dma((ITERS,)),
-                dma((ITERS,)),
-                dma((ITERS,)),
+                dma,
+                dma((2,)),
+                dma,
+                dma((2,)),
                 pltpu.VMEM((2, sy, depth), f32),
             ],
             compiler_params=pltpu.CompilerParams(
                 collective_id=0,
                 has_side_effects=True,
-                vmem_limit_bytes=44 * 1024 * 1024,
+                vmem_limit_bytes=46 * 1024 * 1024,
             ),
         )(*[pltpu.with_memory_space_constraint(value, pltpu.HBM) for value in inputs])
         return pl.pallas_call(
             functools.partial(finish, float(nx * sx * ny * sy * depth)),
             out_shape=(model, model, jax.ShapeDtypeStruct((ITERS,), f32)),
             in_specs=[vmem] * 7,
-            out_specs=(pl.BlockSpec(memory_space=pl.ANY),) * 2 + (smem,),
+            out_specs=(pl.BlockSpec(memory_space=pl.ANY),) * 3,
             scratch_shapes=[
                 pltpu.VMEM((sx, sy, depth), f32),
                 pltpu.VMEM((sx, sy, depth), f32),
-                dma((16,)),
+                pltpu.SMEM((ITERS,), f32),
+                dma((3,)),
             ],
             compiler_params=pltpu.CompilerParams(vmem_limit_bytes=8 * 1024 * 1024),
         )(*last)

time: 50.1 us -> 48.7 us (0.972)
  Pallas kernels: 49.4 us -> 48 us
    pallas_call x1, Pallas kernels: 47.3 us -> 46.5 us  [local(): pl.pallas_call(functools.partial(kernel, nx, ny), out_shape=(model,) * 6...]
    pallas_call x1, Pallas kernels: 2.1 us -> 1.47 us  [local(): pl.pallas_call(functools.partial(finish, float(nx * sx * ny * sy * depth)...]
where the time goes in v5:
time: 48.7 us; the launch traced here: 48.6 us
  Pallas kernels  48 us (99%)
  between operations  0.64 us (1%)
    pallas_call x1, Pallas kernels, local(): pl.pallas_call(functools.partial(kernel, nx, ny), out_shape=(model,) * 6...  46.5 us
    pallas_call x1, Pallas kernels, local(): pl.pallas_call(functools.partial(finish, float(nx * sx * ny * sy * depth)...  1.47 us

profile of v5, /device:TPU:1, one launch (start us, length us, event | category | flops | bytes accessed | tf_op | source)
XLA Modules:
  0.0 48.6 jit_solution(12231818241383959251)
XLA Ops:
  0.6 46.5 %shard_map.94 = (f32[64,32,128]{2,1,0:T(8,128)S(1)}, f32[64,32,128]{2,1,0:T(8,128)S(1)}, f32[64,32,128]{2,1,0:T(8,128)S(1)}, f32[64,32,128]{2,1,0:T(8,128)S(1)},...) custom-call(f32[64,32,128]{2,1,0:T(8,128)} %density.1, f32[64,32,128]{2,1,0:T(8,128)} %slowness.1, ...), custom_call_target="tpu_custom_call" | custom-call | tf_op jit(solution)/shard_map/pallas_call | solution.py:718
  47.2 1.5 %shard_map.95 = (f32[64,32,128]{2,1,0:T(8,128)}, f32[64,32,128]{2,1,0:T(8,128)}, f32[3]{0:T(128)}) custom-call(f32[64,32,128]{2,1,0:T(8,128)S(1)} %get-tuple-element.10.density, f32[64,32,128]{2,1,0:T(8,128)S(1)} %get-tuple-element.11.pull, f32[64,32,128]{2,1,0:T(8,128)S(1)} %get-tuple-element.12.lower, f32[64,32,128]{2,1,0:T(8,128)S(1)} %get-tuple-element.13.upper, ...), custom_call_target="tpu_custom_call" | custom-call | tf_op jit(solution)/shard_map/pallas_call | solution.py:761

commit v6 on v5

--- a/solution.py
+++ b/solution.py
@@ -70,7 +70,7 @@
             slowness_new[x] = slowness[x] - step_slowness * push[x]
             return carry
 
-        lax.fori_loop(k * length, (k + 1) * length, body, 0, unroll=2)
+        lax.fori_loop(k * length, (k + 1) * length, body, 0, unroll=4)
         for source, target, done in pairs:
             pltpu.make_async_copy(source.at[span], target.at[span], done).start()
     lane = lax.broadcasted_iota(jnp.int32, (1, lines.shape[-1]), 1)

time: 48.7 us -> 48.7 us (level)
  no operation moved by 1% of the time
where the time goes in v6:
time: 48.7 us; the launch traced here: 48.6 us
  Pallas kernels  48 us (99%)
  between operations  0.64 us (1%)
    pallas_call x1, Pallas kernels, local(): pl.pallas_call(functools.partial(kernel, nx, ny), out_shape=(model,) * 6...  46.5 us
    pallas_call x1, Pallas kernels, local(): pl.pallas_call(functools.partial(finish, float(nx * sx * ny * sy * depth)...  1.47 us

profile of v6, /device:TPU:1, one launch (start us, length us, event | category | flops | bytes accessed | tf_op | source)
XLA Modules:
  0.0 48.6 jit_solution(168191189172628932)
XLA Ops:
  0.6 46.5 %shard_map.94 = (f32[64,32,128]{2,1,0:T(8,128)S(1)}, f32[64,32,128]{2,1,0:T(8,128)S(1)}, f32[64,32,128]{2,1,0:T(8,128)S(1)}, f32[64,32,128]{2,1,0:T(8,128)S(1)},...) custom-call(f32[64,32,128]{2,1,0:T(8,128)} %density.1, f32[64,32,128]{2,1,0:T(8,128)} %slowness.1, ...), custom_call_target="tpu_custom_call" | custom-call | tf_op jit(solution)/shard_map/pallas_call | solution.py:718
  47.2 1.5 %shard_map.95 = (f32[64,32,128]{2,1,0:T(8,128)}, f32[64,32,128]{2,1,0:T(8,128)}, f32[3]{0:T(128)}) custom-call(f32[64,32,128]{2,1,0:T(8,128)S(1)} %get-tuple-element.10.density, f32[64,32,128]{2,1,0:T(8,128)S(1)} %get-tuple-element.11.pull, f32[64,32,128]{2,1,0:T(8,128)S(1)} %get-tuple-element.12.lower, f32[64,32,128]{2,1,0:T(8,128)S(1)} %get-tuple-element.13.upper, ...), custom_call_target="tpu_custom_call" | custom-call | tf_op jit(solution)/shard_map/pallas_call | solution.py:761
